TPU v7x, 8 devices: a whole 2x2x1 slice. The times are simulated.
8 devices in a mesh: dp: 1 (over z), ep: 8 (over y, x, core).
Axes of the slice: x: 2, y: 2, z: 1, core: 2. Of those that a mesh axis runs over, the one named last changes fastest.
Arguments:
- tok_in: bfloat16 [1024, 2048], P(('dp', 'ep'))
- lat_cache: bfloat16 [1024, 128, 512], P(('dp', 'ep'))
- rope_cache: bfloat16 [1024, 128, 64], P(('dp', 'ep'))
- tok_pos: int32 [1024], P(('dp', 'ep'))
- expert_ids: int32 [1024, 6], P(('dp', 'ep'))
- attn_gain: bfloat16 [2048], replicated
- w_query: bfloat16 [2048, 3072], replicated
- w_kvdown: bfloat16 [2048, 576], replicated
- w_ukey: bfloat16 [16, 128, 512], replicated
- w_uval: bfloat16 [16, 512, 128], replicated
- w_out: bfloat16 [2048, 2048], replicated
- ffn_gain: bfloat16 [2048], replicated
- w_router: bfloat16 [2048, 64], replicated
- sh_gate: bfloat16 [2048, 2816], replicated
- sh_up: bfloat16 [2048, 2816], replicated
- sh_down: bfloat16 [2816, 2048], replicated
- ex_gate: bfloat16 [64, 2048, 1408], P('ep')
- ex_up: bfloat16 [64, 2048, 1408], P('ep')
- ex_down: bfloat16 [64, 1408, 2048], P('ep')
Outputs:
- output 1: bfloat16 [1024, 2048], P(('dp', 'ep'))
- output 2: bfloat16 [1024, 128, 512], P(('dp', 'ep'))
- output 3: bfloat16 [1024, 128, 64], P(('dp', 'ep'))
All inputs are finite; a program needn't handle non-finite values.
Results may differ from a plain program's by a relative error of at most 0.0131528.
Values are sent between devices in bfloat16 or wider.
A program may use at most 1 GiB of HBM per device.

v0:
```python
import jax
import jax.numpy as jnp
from jax import lax
from jax.sharding import PartitionSpec as P

ROUTE_SCALE = 2.827
ROPE_BASE = 10000.0
NORM_EPS = 1e-6


def unit_norm(values):
    mean_sq = jnp.mean(jnp.square(values), axis=-1, keepdims=True)
    return values * lax.rsqrt(mean_sq + NORM_EPS)


def rms_norm(values, gain_vec):
    return unit_norm(values) * gain_vec.astype(jnp.float32)


def rope_rotate(values, angle_rad):
    half_dim = values.shape[-1] // 2
    x_first = values[..., :half_dim]
    x_second = values[..., half_dim:]
    cos_part = jnp.cos(angle_rad)
    sin_part = jnp.sin(angle_rad)
    return jnp.concatenate([x_first * cos_part - x_second * sin_part, x_second * cos_part + x_first * sin_part], axis=-1)


def attention_block(tok_in, lat_cache, rope_cache, tok_pos, attn_gain, w_query, w_kvdown, w_ukey, w_uval, w_out, ffn_gain):
    num_heads, nope_dim, kv_rank = w_ukey.shape
    rope_dim = rope_cache.shape[-1]
    seq_len = lat_cache.shape[1]
    tok_rows = tok_in.shape[0]
    x_wide = tok_in.astype(jnp.float32)
    x_norm = rms_norm(x_wide, attn_gain).astype(jnp.bfloat16)
    q_all = jnp.dot(x_norm, w_query, preferred_element_type=jnp.float32).astype(jnp.bfloat16).reshape(tok_rows, num_heads, nope_dim + rope_dim)
    kv_all = jnp.dot(x_norm, w_kvdown, preferred_element_type=jnp.float32)
    inv_freq = ROPE_BASE ** (-(2.0 * jnp.arange(rope_dim // 2)) / rope_dim)
    angle_rad = tok_pos.astype(jnp.float32)[:, None] * inv_freq[None, :]
    lat_new = unit_norm(kv_all[:, :kv_rank]).astype(jnp.bfloat16)
    rope_new = rope_rotate(kv_all[:, kv_rank:], angle_rad).astype(jnp.bfloat16)
    q_rope = rope_rotate(q_all[:, :, nope_dim:].astype(jnp.float32), angle_rad[:, None, :]).astype(jnp.bfloat16)
    q_lat = jnp.einsum('bhn,hnc->bhc', q_all[:, :, :nope_dim], w_ukey, preferred_element_type=jnp.float32).astype(jnp.bfloat16)
    seq_ids = jnp.arange(seq_len)
    at_pos = (seq_ids[None, :] == tok_pos[:, None])[:, :, None]
    lat_out = jnp.where(at_pos, lat_new[:, None, :], lat_cache)
    rope_out = jnp.where(at_pos, rope_new[:, None, :], rope_cache)
    scores = jnp.einsum('bhc,bsc->bhs', q_lat, lat_out, preferred_element_type=jnp.float32)
    scores = scores + jnp.einsum('bhr,bsr->bhs', q_rope, rope_out, preferred_element_type=jnp.float32)
    scores = scores * (nope_dim + rope_dim) ** -0.5
    visible = (seq_ids[None, :] <= tok_pos[:, None])[:, None, :]
    scores = jnp.where(visible, scores, -jnp.inf)
    prob_mat = jax.nn.softmax(scores, axis=-1).astype(jnp.bfloat16)
    o_lat = jnp.einsum('bhs,bsc->bhc', prob_mat, lat_out, preferred_element_type=jnp.float32).astype(jnp.bfloat16)
    o_heads = jnp.einsum('bhc,hcv->bhv', o_lat, w_uval, preferred_element_type=jnp.float32).astype(jnp.bfloat16)
    attn_out = jnp.dot(o_heads.reshape(tok_rows, -1), w_out, preferred_element_type=jnp.float32)
    resid_bf = (x_wide + attn_out).astype(jnp.bfloat16)
    h_norm = rms_norm(resid_bf.astype(jnp.float32), ffn_gain).astype(jnp.bfloat16)
    return resid_bf, h_norm, lat_out, rope_out


def route_weights(h_norm, w_router, expert_ids):
    num_experts = w_router.shape[1]
    gate_prob = jax.nn.sigmoid(jnp.dot(h_norm, w_router, preferred_element_type=jnp.float32))
    pick_mask = expert_ids[:, :, None] == jnp.arange(num_experts)[None, None, :]
    chosen = jnp.sum(jnp.where(pick_mask, gate_prob[:, None, :], 0.0), axis=-1)
    route_w = ROUTE_SCALE * chosen / jnp.sum(chosen, axis=1, keepdims=True)
    return route_w, pick_mask


def swiglu_shared(h_norm, sh_gate, sh_up, sh_down):
    gate_val = jnp.dot(h_norm, sh_gate, preferred_element_type=jnp.float32)
    up_val = jnp.dot(h_norm, sh_up, preferred_element_type=jnp.float32)
    act_val = (jax.nn.silu(gate_val) * up_val).astype(jnp.bfloat16)
    return jnp.dot(act_val, sh_down, preferred_element_type=jnp.float32)


def solution(mesh):
    ep_size = mesh.shape['ep']
    row_one = P(('dp', 'ep'))
    row_two = P(('dp', 'ep'), None)
    row_three = P(('dp', 'ep'), None, None)
    rep_one = P(None)
    rep_two = P(None, None)
    rep_three = P(None, None, None)
    exp_spec = P('ep', None, None)

    def local_step(tok_in, lat_cache, rope_cache, tok_pos, expert_ids, attn_gain, w_query, w_kvdown, w_ukey, w_uval, w_out, ffn_gain, w_router, sh_gate, sh_up, sh_down, ex_gate, ex_up, ex_down):
        resid_bf, h_norm, lat_out, rope_out = attention_block(tok_in, lat_cache, rope_cache, tok_pos, attn_gain, w_query, w_kvdown, w_ukey, w_uval, w_out, ffn_gain)
        route_w, pick_mask = route_weights(h_norm, w_router, expert_ids)
        shared_out = swiglu_shared(h_norm, sh_gate, sh_up, sh_down)
        tok_rows, top_k = expert_ids.shape
        num_experts = w_router.shape[1]
        local_experts = ex_gate.shape[0]
        d_model = h_norm.shape[1]
        cap_slots = max(2, -(-2 * tok_rows * top_k // num_experts))
        pick_int = pick_mask.astype(jnp.int32)
        per_tok = jnp.sum(pick_int, axis=1)
        before = jnp.cumsum(per_tok, axis=0) - per_tok
        slot_idx = jnp.sum(pick_int * before[:, None, :], axis=-1)
        slot_hot = slot_idx[:, :, None] == jnp.arange(cap_slots)
        place_hot = (pick_mask[:, :, :, None] & slot_hot[:, :, None, :]).astype(jnp.bfloat16)
        place_tok = jnp.sum(place_hot, axis=1)
        send_rows = jnp.einsum('tec,td->ecd', place_tok, h_norm, preferred_element_type=jnp.float32).astype(jnp.bfloat16)
        send_rows = send_rows.reshape(ep_size, local_experts, cap_slots, d_model)
        recv_rows = lax.all_to_all(send_rows, 'ep', 0, 2, tiled=True)
        recv_rows = recv_rows.reshape(local_experts, ep_size * cap_slots, d_model)
        gate_val = jnp.einsum('emd,edf->emf', recv_rows, ex_gate, preferred_element_type=jnp.float32)
        up_val = jnp.einsum('emd,edf->emf', recv_rows, ex_up, preferred_element_type=jnp.float32)
        act_val = (jax.nn.silu(gate_val) * up_val).astype(jnp.bfloat16)
        exp_out = jnp.einsum('emf,efd->emd', act_val, ex_down, preferred_element_type=jnp.float32).astype(jnp.bfloat16)
        exp_out = exp_out.reshape(1, local_experts, ep_size * cap_slots, d_model)
        back_rows = lax.all_to_all(exp_out, 'ep', 2, 0, tiled=True)
        back_rows = back_rows.reshape(num_experts, cap_slots, d_model)
        picked = jnp.einsum('tkec,ecd->tkd', place_hot, back_rows, preferred_element_type=jnp.float32)
        routed = jnp.sum(route_w[:, :, None] * picked, axis=1)
        out_hidden = (resid_bf.astype(jnp.float32) + shared_out + routed).astype(jnp.bfloat16)
        return out_hidden, lat_out, rope_out

    in_specs = (row_two, row_three, row_three, row_one, row_two, rep_one, rep_two, rep_two, rep_three, rep_three, rep_two, rep_one, rep_two, rep_two, rep_two, rep_two, exp_spec, exp_spec, exp_spec)
    out_specs = (row_two, row_three, row_three)
    return jax.shard_map(local_step, mesh=mesh, in_specs=in_specs, out_specs=out_specs, check_vma=False)
```

profile of v0, /device:TPU:0, one launch (start us, length us, event | category | flops | bytes accessed | tf_op | source)
XLA Modules:
  0.0 323.7 jit_solution(17533242265522205240)
XLA Ops:
  0.6 0.0 copy-start
  0.7 0.8 convert_element_type.96
  1.5 0.7 iota_compare_fusion.3
  2.2 0.7 convert_reduce_fusion
  2.9 0.7 iota_compare_fusion
  3.7 0.7 convert_element_type.89
  4.3 1.2 fusion.41
  5.6 0.0 copy-done
  5.6 1.9 fusion.52
  7.5 0.1 multiply_reduce_fusion.1
  7.6 0.1 multiply_cosine_fusion
  7.7 0.1 copy.45
  7.8 0.1 copy.46
  7.9 6.7 %convolution_convert_fusion.1 = bf16[128,3072]{1,0:T(8,128)(2,1)S(1)} fusion(bf16[2048,3072]{1,0:T(8,128)(2,1)} %param.25, bf16[128,2048]{1,0:T(8,128)(2,1)} %param.19, f32[2048]{0:T(1024)S(1)} %convert_element_type.89, f32[128]{0:T(128)S(1)} %add_rsqrt_fusion.2), kind=kOutput, calls=%fused_computation.15 | convolution fusion | flops 1612054528 | bytes 13902336 | tf_op jit(solution)/shard_map/dot_general | solution.py:36
  14.6 0.4 copy.40
  15.0 0.4 copy.60
  15.5 0.1 convert_element_type.95
  15.5 0.1 copy.47
  15.7 0.1 copy.42
  15.8 3.7 %convert_bitcast_fusion.1 = bf16[128,16,512]{2,0,1:T(8,128)(2,1)} fusion(bf16[16,128,512]{2,1,0:T(8,128)(2,1)} %param.27, bf16[128,16,192]{0,2,1:T(8,128)(2,1)S(1)} %bitcast.65), kind=kOutput, calls=%fused_computation.30 | convolution fusion | flops 269484032 | bytes 4718592 | tf_op jit(solution)/shard_map/bhn,hnc->bhc/dot_general | solution.py:43
  19.5 2.7 broadcast_select_fusion.1
  22.3 0.0 copy-start.3
  22.3 15.2 %broadcast_select_fusion = bf16[128,128,512]{2,1,0:T(8,128)(2,1)} fusion(bf16[128,128,512]{2,1,0:T(8,128)(2,1)} %param.20, pred[128,128]{1,0:T(8,128)(4,1)S(1)} %get-tuple-element.14, bf16[128,512]{1,0:T(8,128)(2,1)S(1)} %copy.42), kind=kLoop, calls=%fused_computation.1 | loop fusion | flops 8388608 | bytes 33701888 | tf_op jit(solution)/shard_map/jit(_where)/select_n | solution.py:46
  37.5 0.5 subtract_convert_fusion
  38.0 0.0 copy-done.3
  38.0 0.7 fusion.45
  38.8 10.9 %fusion.32 = f32[128,16,128]{2,1,0:T(8,128)S(1)} fusion(f32[128,16,128]{2,1,0:T(8,128)S(1)} %fusion.45, bf16[128,128,512]{2,1,0:T(8,128)(2,1)} %broadcast_select_fusion, bf16[128,16,512]{2,0,1:T(8,128)(2,1)} %convert_bitcast_fusion.1, pred[128,128]{1,0:T(8,128)(4,1)S(1)} %get-tuple-element.13), kind=kOutput, calls=%fused_computation.39 | convolution fusion | flops 269221888 | bytes 20987904 | tf_op jit(solution)/shard_map/bhc,bsc->bhs/dot_general | solution.py:48
  49.7 0.6 fusion.60
  50.3 0.0 copy-start.2
  50.3 12.3 %convolution_convert_fusion.2 = bf16[128,16,512]{2,1,0:T(8,128)(2,1)} fusion(bf16[128,128,512]{2,1,0:T(8,128)(2,1)} %broadcast_select_fusion, f32[128,16]{1,0:T(8,128)S(1)} %fusion.60, f32[128,16,128]{2,1,0:T(8,128)S(1)} %fusion.32), kind=kOutput, calls=%fused_computation.32 | convolution fusion | flops 270272640 | bytes 19931136 | tf_op jit(solution)/shard_map/bhs,bsc->bhc/dot_general | solution.py:54
  62.6 4.9 %fusion.35 = bf16[16,128,128]{1,2,0:T(8,128)(2,1)S(1)} fusion(bf16[16,512,128]{2,1,0:T(8,128)(2,1)} %param.28, bf16[128,16,512]{2,1,0:T(8,128)(2,1)} %convolution_convert_fusion.2), kind=kOutput, calls=%fused_computation.40 | convolution fusion | flops 268697600 | bytes 4718592 | tf_op jit(solution)/shard_map/bhc,hcv->bhv/dot_general | solution.py:55
  67.5 0.0 copy-done.2
  67.5 0.0 copy-start.5
  67.5 0.0 copy-start.6
  67.6 4.7 %multiply_reduce_fusion = (f32[128]{0:T(128)S(1)}, f32[128,2048]{1,0:T(8,128)S(1)}) fusion(bf16[128,2048]{0,1:T(8,128)(2,1)S(1)} %bitcast.66, bf16[2048,2048]{1,0:T(8,128)(2,1)} %param.29, bf16[128,2048]{1,0:T(8,128)(2,1)S(1)} %copy-done.2), kind=kOutput, calls=%fused_computation.49 | convolution fusion | flops 1075314560 | bytes 10486272 | tf_op jit(solution)/shard_map/dot_general | solution.py:56
  72.3 0.1 copy.50
  72.4 0.2 reduce_window_sum.11
  72.6 0.1 copy.52
  72.7 0.0 copy-done.5
  72.8 0.0 copy-done.6
  72.8 0.5 fusion.13
  73.3 1.9 convolution_convert_fusion
  75.2 75.8 %all_to_all.30 = bf16[8,8,24,2048]{3,2,1,0:T(8,128)(2,1)S(1)} all-to-all(bf16[8,8,24,2048]{3,2,1,0:T(8,128)(2,1)S(1)} %bitcast.60), channel_id=1, replica_groups=mesh['dp'=1,'ep'=8] {'ep'}, dimensions={0} | all-to-all | bytes 12582912 | tf_op jit(solution)/shard_map/all_to_all | solution.py:106
  151.0 3.3 %copy.54 = bf16[1,8,8,24,2048]{4,3,2,1,0:T(8,128)(2,1)} copy(bf16[1,8,8,24,2048]{4,3,1,2,0:T(8,128)(2,1)S(1)} %bitcast.61) | data formatting | bytes 12582912 | tf_op jit(solution)/shard_map/all_to_all | solution.py:106
  154.2 22.2 %fusion.61 = f32[8,192,1408]{2,1,0:T(8,128)} fusion(bf16[8,192,2048]{2,1,0:T(8,128)(2,1)} %bitcast.62, bf16[8,2048,1408]{2,1,0:T(8,128)(2,1)} %param.35), kind=kOutput, calls=%fused_computation.88 | convolution fusion | flops 8858370048 | bytes 61079552 | tf_op jit(solution)/shard_map/emd,edf->emf/dot_general | solution.py:108
  176.5 24.9 %multiply_convert_fusion.clone.6 = bf16[8,192,1408]{2,1,0:T(8,128)(2,1)} fusion(f32[8,192,1408]{2,1,0:T(8,128)} %fusion.61, bf16[8,192,2048]{2,1,0:T(8,128)(2,1)} %bitcast.63, bf16[8,2048,1408]{2,1,0:T(8,128)(2,1)} %param.36), kind=kOutput, calls=%fused_computation.2.clone.clone.clone.clone.clone.1 | convolution fusion | flops 8871346176 | bytes 65404928 | tf_op jit(solution)/shard_map/emd,edf->emf/dot_general | solution.py:109
  201.4 18.9 %convert_bitcast_fusion = bf16[1,8,192,2048]{3,2,1,0:T(8,128)(2,1)S(1)} fusion(bf16[8,1408,2048]{2,1,0:T(8,128)(2,1)} %param.37, bf16[8,192,1408]{2,1,0:T(8,128)(2,1)} %multiply_convert_fusion.clone.6), kind=kOutput, calls=%fused_computation.8 | convolution fusion | flops 8861515776 | bytes 56754176 | tf_op jit(solution)/shard_map/emf,efd->emd/dot_general | solution.py:111
  220.3 6.1 %copy.55 = bf16[1,8,192,2048]{3,1,0,2:T(8,128)(2,1)} copy(bf16[1,8,192,2048]{3,2,1,0:T(8,128)(2,1)S(1)} %convert_bitcast_fusion) | data formatting | bytes 12582912 | tf_op jit(solution)/shard_map/reshape | solution.py:112
  226.4 0.0 copy-start.4
  226.4 3.6 %all-to-all-start.1 = ((bf16[1,8,192,2048]{3,1,0,2:T(8,128)(2,1)}), bf16[1,8,192,2048]{3,1,0,2:T(8,128)(2,1)}, u32[]{:S(2)}, u32[]{:S(2)}) async-start(bf16[1,8,192,2048]{3,1,0,2:T(8,128)(2,1)} %copy.55), calls=%async_computation.1 | async-start | bytes 12582912 | tf_op jit(solution)/shard_map/all_to_all | solution.py:113
  230.0 0.0 copy-done.4
  230.0 0.4 fusion.40
  230.4 0.1 select_reduce_fusion
  230.5 7.2 %fusion.59 = f32[128,2816]{1,0:T(8,128)} fusion(bf16[2048,2816]{1,0:T(8,128)(2,1)} %param.32, f32[128,2048]{1,0:T(8,128)S(1)} %get-tuple-element.16, f32[2048]{0:T(1024)S(1)} %convert_element_type.104, f32[128]{0:T(128)S(1)} %add_rsqrt_fusion), kind=kOutput, calls=%fused_computation.86 | convolution fusion | flops 1477181440 | bytes 14033408 | tf_op jit(solution)/shard_map/dot_general | solution.py:72
  237.7 63.8 %all-to-all-done.1 = bf16[1,8,192,2048]{3,1,0,2:T(8,128)(2,1)} async-done(((bf16[1,8,192,2048]{3,1,0,2:T(8,128)(2,1)}), bf16[1,8,192,2048]{3,1,0,2:T(8,128)(2,1)}, u32[]{:S(2)}, u32[]{:S(2)}) %all-to-all-start.1) | async-done | bytes 6291488 | tf_op jit(solution)/shard_map/all_to_all | solution.py:113
  301.5 9.3 %fusion.3 = f32[128,2048]{1,0:T(8,128)} fusion(f32[128,6]{0,1:T(8,128)S(1)} %multiply_divide_fusion, bf16[1,8,8,24,2048]{4,1,3,2,0:T(8,128)(2,1)} %bitcast.10, pred[128,6,24]{0,2,1:T(8,128)(4,1)S(1)} %iota_compare_fusion.1, pred[128,6,64]{0,2,1:T(8,128)(4,1)S(1)} %iota_compare_fusion), kind=kOutput, calls=%fused_computation.6 | convolution fusion | flops 4835901440 | bytes 7410688 | tf_op jit(solution)/shard_map/tkec,ecd->tkd/dot_general | solution.py:115
  310.8 0.0 copy-start.1
  310.8 12.7 %fusion.12 = bf16[128,2048]{1,0:T(8,128)(2,1)} fusion(f32[128,2048]{1,0:T(8,128)} %fusion.3, f32[128,2048]{1,0:T(8,128)S(1)} %get-tuple-element.16, bf16[2816,2048]{1,0:T(8,128)(2,1)} %param.34, bf16[2048,2816]{1,0:T(8,128)(2,1)} %param.33, f32[128,2816]{1,0:T(8,128)} %fusion.59, f32[2048]{0:T(1024)S(1)} %convert_element_type.104, f32[128]{0:T(128)S(1)} %add_rsqrt_fusion), kind=kOutput, calls=%fused_computation.22 | convolution fusion | flops 2956525568 | bytes 27140608 | tf_op jit(solution)/shard_map/dot_general | solution.py:75
  323.5 0.0 copy-done.1
  (12 shorter events, 0.1 us)
Async XLA Ops:
  0.6 5.0 %copy-start = (bf16[2048,576]{0,1:T(8,128)(2,1)S(1)}, bf16[2048,576]{0,1:T(8,128)(2,1)}, u32[]{:S(2)}) copy-start(bf16[2048,576]{0,1:T(8,128)(2,1)} %param.26) | copy-start | bytes 7077892
  22.3 15.7 %copy-start.3 = (bf16[128,128,64]{1,2,0:T(8,128)(2,1)}, bf16[128,128,64]{1,2,0:T(8,128)(2,1)S(1)}, u32[]{:S(2)}) copy-start(bf16[128,128,64]{1,2,0:T(8,128)(2,1)S(1)} %broadcast_select_fusion.1) | copy-start | bytes 6291460
  50.3 17.2 %copy-start.2 = (bf16[128,2048]{1,0:T(8,128)(2,1)S(1)}, bf16[128,2048]{1,0:T(8,128)(2,1)}, u32[]{:S(2)}) copy-start(bf16[128,2048]{1,0:T(8,128)(2,1)} %param.19) | copy-start | bytes 1572868
  67.5 5.2 %copy-start.5 = (s32[128,6]{0,1:T(8,128)S(1)}, s32[128,6]{0,1:T(8,128)}, u32[]{:S(2)}) copy-start(s32[128,6]{0,1:T(8,128)} %param.23) | copy-start | bytes 9220
  67.5 5.2 %copy-start.6 = (bf16[2048]{0:T(1024)(128)(2,1)S(1)}, bf16[2048]{0:T(1024)(128)(2,1)}, u32[]{:S(2)}) copy-start(bf16[2048]{0:T(1024)(128)(2,1)} %param.30) | copy-start | bytes 12292
  226.4 3.6 %copy-start.4 = (bf16[2048,64]{0,1:T(8,128)(2,1)S(1)}, bf16[2048,64]{0,1:T(8,128)(2,1)}, u32[]{:S(2)}) copy-start(bf16[2048,64]{0,1:T(8,128)(2,1)} %param.31) | copy-start | bytes 786436
  226.4 75.1 %all-to-all-start.1 = ((bf16[1,8,192,2048]{3,1,0,2:T(8,128)(2,1)}), bf16[1,8,192,2048]{3,1,0,2:T(8,128)(2,1)}, u32[]{:S(2)}, u32[]{:S(2)}) async-start(bf16[1,8,192,2048]{3,1,0,2:T(8,128)(2,1)} %copy.55), calls=%async_computation.1 | async-start | bytes 12582912 | tf_op jit(solution)/shard_map/all_to_all | solution.py:113
  310.8 12.7 %copy-start.1 = (bf16[2048,576]{0,1:T(8,128)(2,1)S(1)}, bf16[2048,576]{0,1:T(8,128)(2,1)}, u32[]{:S(2)}) copy-start(bf16[2048,576]{0,1:T(8,128)(2,1)} %param.26) | copy-start | bytes 7077892
where the time goes:
time: 328 us; the launch traced here: 324 us
  matrix products  143 us (44%)
  blocking collectives  75.8 us (23%)
  waiting for transfers between devices  63.8 us (19%)
  other arithmetic  25.2 us (8%)
  local copies, waits for them, and re-layouts  10.8 us (3%)
  starting transfers between devices  3.6 us (1%)
    all_to_all x1, blocking collectives, local_step(): recv_rows = lax.all_to_all(send_rows, 'ep', 0, 2, tiled=True)  75.8 us
    all_to_all x1, waiting for transfers between devices, local_step(): back_rows = lax.all_to_all(exp_out, 'ep', 2, 0, tiled=True)  63.8 us
    dot_general x1, matrix products, local_step(): jnp.einsum('emd,edf->emf', recv_rows, ex_up, preferred_element_type=jnp.f...  24.9 us
    dot_general x1, matrix products, local_step(): jnp.einsum('emd,edf->emf', recv_rows, ex_gate, preferred_element_type=jnp...  22.2 us
    dot_general x1, matrix products, local_step(): jnp.einsum('emf,efd->emd', act_val, ex_down, preferred_element_type=jnp.f...  18.9 us
    select_n x1, other arithmetic, attention_block(): lat_out = jnp.where(at_pos, lat_new[:, None, :], lat_cache)  15.2 us
    dot_general x1, matrix products, swiglu_shared(): return jnp.dot(act_val, sh_down, preferred_element_type=jnp.float32)  12.7 us
    dot_general x1, matrix products, attention_block(): jnp.einsum('bhs,bsc->bhc', prob_mat, lat_out, preferred_element_type=jnp....  12.3 us
  transfers between devices with their start and end apart: 1, of which 1 were waited for; matrix products, arithmetic and copies ran while one was open for 2% of the time, Pallas kernels for 0%

commit v1 on v0

v1 whole, which is shorter than its diff:
```python
import functools

import jax
import jax.numpy as jnp
from jax import lax
from jax.experimental import pallas as pl
from jax.experimental.pallas import tpu as pltpu
from jax.sharding import PartitionSpec as P

ROUTE_SCALE = 2.827
ROPE_BASE = 10000.0
NORM_EPS = 1e-6
CAP = 24
CHUNK = 256
F32 = jnp.float32
BF16 = jnp.bfloat16


def unit_norm(values):
    mean_sq = jnp.mean(jnp.square(values), axis=-1, keepdims=True)
    return values * lax.rsqrt(mean_sq + NORM_EPS)


def rms_norm(values, gain_vec):
    return unit_norm(values) * gain_vec.astype(jnp.float32)


def rope_rotate(values, angle_rad):
    half_dim = values.shape[-1] // 2
    x_first = values[..., :half_dim]
    x_second = values[..., half_dim:]
    cos_part = jnp.cos(angle_rad)
    sin_part = jnp.sin(angle_rad)
    return jnp.concatenate([x_first * cos_part - x_second * sin_part, x_second * cos_part + x_first * sin_part], axis=-1)


def attention_block(tok_in, lat_cache, rope_cache, tok_pos, attn_gain, w_query, w_kvdown, w_ukey, w_uval, w_out, ffn_gain):
    num_heads, nope_dim, kv_rank = w_ukey.shape
    rope_dim = rope_cache.shape[-1]
    seq_len = lat_cache.shape[1]
    tok_rows = tok_in.shape[0]
    x_wide = tok_in.astype(jnp.float32)
    x_norm = rms_norm(x_wide, attn_gain).astype(jnp.bfloat16)
    q_all = jnp.dot(x_norm, w_query, preferred_element_type=jnp.float32).astype(jnp.bfloat16).reshape(tok_rows, num_heads, nope_dim + rope_dim)
    kv_all = jnp.dot(x_norm, w_kvdown, preferred_element_type=jnp.float32)
    inv_freq = ROPE_BASE ** (-(2.0 * jnp.arange(rope_dim // 2)) / rope_dim)
    angle_rad = tok_pos.astype(jnp.float32)[:, None] * inv_freq[None, :]
    lat_new = unit_norm(kv_all[:, :kv_rank]).astype(jnp.bfloat16)
    rope_new = rope_rotate(kv_all[:, kv_rank:], angle_rad).astype(jnp.bfloat16)
    q_rope = rope_rotate(q_all[:, :, nope_dim:].astype(jnp.float32), angle_rad[:, None, :]).astype(jnp.bfloat16)
    q_lat = jnp.einsum('bhn,hnc->bhc', q_all[:, :, :nope_dim], w_ukey, preferred_element_type=jnp.float32).astype(jnp.bfloat16)
    seq_ids = jnp.arange(seq_len)
    at_pos = (seq_ids[None, :] == tok_pos[:, None])[:, :, None]
    lat_out = jnp.where(at_pos, lat_new[:, None, :], lat_cache)
    rope_out = jnp.where(at_pos, rope_new[:, None, :], rope_cache)
    scores = jnp.einsum('bhc,bsc->bhs', q_lat, lat_out, preferred_element_type=jnp.float32)
    scores = scores + jnp.einsum('bhr,bsr->bhs', q_rope, rope_out, preferred_element_type=jnp.float32)
    scores = scores * (nope_dim + rope_dim) ** -0.5
    visible = (seq_ids[None, :] <= tok_pos[:, None])[:, None, :]
    scores = jnp.where(visible, scores, -jnp.inf)
    prob_mat = jax.nn.softmax(scores, axis=-1).astype(jnp.bfloat16)
    o_lat = jnp.einsum('bhs,bsc->bhc', prob_mat, lat_out, preferred_element_type=jnp.float32).astype(jnp.bfloat16)
    o_heads = jnp.einsum('bhc,hcv->bhv', o_lat, w_uval, preferred_element_type=jnp.float32).astype(jnp.bfloat16)
    attn_out = jnp.dot(o_heads.reshape(tok_rows, -1), w_out, preferred_element_type=jnp.float32)
    resid_bf = (x_wide + attn_out).astype(jnp.bfloat16)
    h_norm = rms_norm(resid_bf.astype(jnp.float32), ffn_gain).astype(jnp.bfloat16)
    return resid_bf, h_norm, lat_out, rope_out


def route_table(h_norm, w_router, expert_ids):
    num_experts = w_router.shape[1]
    gate_prob = jax.nn.sigmoid(jnp.dot(h_norm, w_router, preferred_element_type=jnp.float32))
    picked = jnp.any(expert_ids[:, :, None] == jnp.arange(num_experts)[None, None, :], axis=1)
    chosen = jnp.where(picked, gate_prob, 0.0)
    table = ROUTE_SCALE * chosen / jnp.sum(chosen, axis=1, keepdims=True)
    return table.T


def moe_kernel(h_ref, rw_ref, res_ref, eg, eu, ed, sg, su, sd, out_ref,
               ring, hall, xbuf, actt, actsh, acc, drecv, r1, r2, stage, base, pw, pwf, pbuf, ebuf, rwin,
               ring_sem, ag_s, ag_r, rw_s, rw_r, d_s, d_r, s1_s, s1_r, s2_s, s2_r):
    rows = h_ref.shape[0]
    half = rows // 2
    d_model = h_ref.shape[1]
    ff = eg.shape[2]
    n_exp = eg.shape[0]
    n_chunk = d_model // CHUNK
    grp = 2 * CAP
    mids = [(n, min(CHUNK, ff - n)) for n in range(0, ff, CHUNK)]
    me = lax.axis_index('ep')
    core = me % 2
    cx = (me // 2) % 2
    cy = me // 4
    mate = me + 1 - 2 * core
    xn = me + 2 - 4 * cx
    yn = me + 4 - 8 * cy
    dg = yn + 2 - 4 * cx
    others = [(0, 1, mate), (1, 0, xn), (1, 1, xn + 1 - 2 * core), (2, 0, yn), (2, 1, yn + 1 - 2 * core), (3, 0, dg), (3, 1, dg + 1 - 2 * core)]

    def remote(src, dst, ssem, rsem, dev):
        return pltpu.make_async_remote_copy(src_ref=src, dst_ref=dst, send_sem=ssem, recv_sem=rsem, device_id={'ep': dev}, device_id_type=pl.DeviceIdType.MESH)

    step = d_model // 4

    def pair_copies(slot, gate, up):
        out = []
        for b, src in enumerate((gate, up)):
            for q in range(4):
                out.append(pltpu.make_async_copy(src.at[pl.ds(q * step, step), :], ring.at[slot, b, pl.ds(q * step, step), :], ring_sem.at[slot, b * 4 + q]))
        return out

    def shared_copies(slot, i):
        return pair_copies(slot, sg.at[:, pl.ds(i * ff, ff)], su.at[:, pl.ds(i * ff, ff)])

    def expert_copies(slot, e):
        return pair_copies(slot, eg.at[e], eu.at[e])

    def tile_at(slot, i):
        return ring.at[slot, i // 5, pl.ds(0, ff), pl.ds((i % 5) * CHUNK, CHUNK)]

    def down_copies(slot, j):
        cols = pl.ds(pl.multiple_of(j * CHUNK, CHUNK), CHUNK)
        out = [pltpu.make_async_copy(ed.at[e, :, cols], tile_at(slot, e), ring_sem.at[slot, e]) for e in range(n_exp)]
        for i in range(2):
            out.append(pltpu.make_async_copy(sd.at[pl.ds(i * ff, ff), cols], tile_at(slot, n_exp + i), ring_sem.at[slot, n_exp + i]))
        return out

    def start(copies):
        for c in copies:
            c.start()

    def wait(copies):
        for c in copies:
            c.wait()

    start(shared_copies(0, 0))
    start(shared_copies(1, 1))
    start(expert_copies(2, 0))

    barrier = pltpu.get_barrier_semaphore()
    for _, _, dev in others:
        pl.semaphore_signal(barrier, inc=1, device_id={'ep': dev}, device_id_type=pl.DeviceIdType.MESH)
    pl.semaphore_wait(barrier, len(others))

    part_a, part_b = pl.ds(0, half), pl.ds(half, half)
    own, other = pl.ds(0, rows), pl.ds(rows, rows)
    rw_copies = [remote(rw_ref.at[pl.ds(pl.multiple_of(dev * n_exp, n_exp), n_exp), :], rwin.at[r, p], rw_s.at[i], rw_r.at[i], dev) for i, (r, p, dev) in enumerate(others)]
    start(rw_copies)
    to_mate = remote(h_ref, hall.at[0, other], ag_s.at[0], ag_r.at[0], mate)
    x_a = remote(h_ref.at[part_a], hall.at[1, part_a], ag_s.at[1], ag_r.at[1], xn)
    x_b = remote(h_ref.at[part_b], hall.at[1, part_b], ag_s.at[2], ag_r.at[2], xn)
    y_b = remote(h_ref.at[part_b], hall.at[2, part_b], ag_s.at[3], ag_r.at[3], yn)
    y_a = remote(h_ref.at[part_a], hall.at[2, part_a], ag_s.at[4], ag_r.at[4], yn)
    d_a = remote(hall.at[1, part_a], hall.at[3, part_a], ag_s.at[5], ag_r.at[5], yn)
    d_b = remote(hall.at[2, part_b], hall.at[3, part_b], ag_s.at[6], ag_r.at[6], xn)
    m_x = remote(hall.at[1, own], hall.at[1, other], ag_s.at[7], ag_r.at[7], mate)
    m_y = remote(hall.at[2, own], hall.at[2, other], ag_s.at[8], ag_r.at[8], mate)
    m_d = remote(hall.at[3, own], hall.at[3, other], ag_s.at[9], ag_r.at[9], mate)
    for c in (x_a, y_b, to_mate, x_b, y_a):
        c.start()

    hall[0, 0:rows, :] = h_ref[...]
    rwin[0, 0] = rw_ref[pl.ds(pl.multiple_of(me * n_exp, n_exp), n_exp), :]
    for c in rw_copies:
        c.wait_recv()

    def gather_rows(r):
        both = jnp.concatenate([rwin[r, 0], rwin[r, 1]], axis=1)
        two = 2 * rows
        t_in = lax.broadcasted_iota(jnp.int32, (two, two), 0)
        t_out = lax.broadcasted_iota(jnp.int32, (two, two), 1)
        ahead = jnp.where((t_in < t_out) & ((t_in < rows) == (t_out < rows)), 1.0, 0.0).astype(BF16)
        picked = both > 0.0
        before = jnp.dot(jnp.where(picked, 1.0, 0.0).astype(BF16), ahead, preferred_element_type=F32)
        lane = lax.broadcasted_iota(jnp.int32, (n_exp, two), 1)
        slot = jnp.where(picked, before + jnp.where(lane < rows, 0.0, float(CAP)), -1.0).astype(jnp.int32)
        want = lax.broadcasted_iota(jnp.int32, (grp, two), 0)
        for e in range(n_exp):
            hit = want == slot[e:e + 1, :]
            pbuf[e * grp:(e + 1) * grp, :] = jnp.where(hit, 1.0, 0.0).astype(BF16)
            pwf[e * grp:(e + 1) * grp, :] = jnp.where(hit, both[e:e + 1, :], 0.0)
        wide = 512
        for n in range(0, d_model, wide):
            got = jnp.dot(pbuf[...], hall[r, :, n:n + wide], preferred_element_type=F32).astype(BF16)
            for e in range(n_exp):
                xbuf[e, r * grp:(r + 1) * grp, n:n + wide] = got[e * grp:(e + 1) * grp, :]
        turned = pwf[...].T
        hi = turned.astype(BF16)
        rest = turned - hi.astype(F32)
        mid = rest.astype(BF16)
        pw[r, 0] = hi
        pw[r, 1] = mid
        pw[r, 2] = (rest - mid.astype(F32)).astype(BF16)

    def shared_item(i):
        wait(shared_copies(i, i))
        for n, w in mids:
            g = jnp.dot(h_ref[...], ring[i, 0, :, n:n + w], preferred_element_type=F32)
            u = jnp.dot(h_ref[...], ring[i, 1, :, n:n + w], preferred_element_type=F32)
            actsh[i, :, n:n + w] = (jax.nn.silu(g) * u).astype(BF16)
        start(expert_copies(i, i + 1))

    shared_item(0)
    x_a.wait_recv()
    d_a.start()
    y_b.wait_recv()
    d_b.start()
    to_mate.wait_recv()
    gather_rows(0)
    shared_item(1)
    x_b.wait_recv()
    m_x.start()
    y_a.wait_recv()
    m_y.start()
    m_x.wait_recv()
    gather_rows(1)
    m_y.wait_recv()
    gather_rows(2)
    d_a.wait_recv()
    d_b.wait_recv()
    m_d.start()
    m_d.wait_recv()
    gather_rows(3)

    @pl.loop(0, n_exp)
    def _(e):
        slot = (e + 2) % 3
        wait(expert_copies(slot, e))
        for n, w in mids:
            g = jnp.dot(xbuf[e], ring[slot, 0, :, n:n + w], preferred_element_type=F32)
            u = jnp.dot(xbuf[e], ring[slot, 1, :, n:n + w], preferred_element_type=F32)
            actt[:, n:n + w] = (jax.nn.silu(g) * u).astype(BF16)
        xbuf[e, :, 0:ff] = actt[...]

        @pl.when(e + 3 < n_exp)
        def _():
            start(expert_copies(slot, e + 3))

        @pl.when(e + 3 >= n_exp)
        def _():
            start(down_copies(slot, e + 3 - n_exp))

    def first_stage(j):
        odd = j % 2
        dev = xn + odd * (yn - xn)
        return [remote(acc.at[j, 1 + odd], r1.at[j, 0], s1_s.at[j, 0], s1_r.at[j, 0], dev), remote(acc.at[j, 3], r1.at[j, 1], s1_s.at[j, 1], s1_r.at[j, 1], dev)]

    def second_stage(j):
        odd = j % 2
        dev = yn + odd * (xn - yn)
        return remote(acc.at[j, 2 - odd], r2.at[j], s2_s.at[j], s2_r.at[j], dev)

    def swap(j):
        return remote(stage.at[j % 2], drecv.at[j], d_s.at[j], d_r.at[j], mate)

    def send_sum(j):
        swap(j).wait_recv()
        acc[j] = acc[j] + drecv[j]
        start(first_stage(j))

    @pl.loop(0, n_chunk)
    def _(j):
        slot = (j + n_exp + 2) % 3
        wait(down_copies(slot, j))
        for e in range(n_exp):
            tile = ring[slot, e // 5, 0:ff, (e % 5) * CHUNK:(e % 5 + 1) * CHUNK]
            got = jnp.dot(xbuf[e, :, 0:ff], tile, preferred_element_type=F32).astype(BF16)
            for r in range(4):
                ebuf[r, e * grp:(e + 1) * grp, :] = got[r * grp:(r + 1) * grp, :]

        @pl.when(j >= 2)
        def _():
            swap(j - 2).wait_send()

        for r in range(4):
            part = jnp.dot(pw[r, 0], ebuf[r], preferred_element_type=F32)
            part = part + jnp.dot(pw[r, 1], ebuf[r], preferred_element_type=F32)
            part = part + jnp.dot(pw[r, 2], ebuf[r], preferred_element_type=F32)
            acc[j, r] = part[0:rows, :]
            stage[j % 2, r] = part[rows:, :]
        swap(j).start()

        cols = pl.ds(pl.multiple_of(j * CHUNK, CHUNK), CHUNK)
        total = res_ref[:, cols].astype(F32)
        for i in range(2):
            k = n_exp + i
            tile = ring[slot, k // 5, 0:ff, (k % 5) * CHUNK:(k % 5 + 1) * CHUNK]
            total = total + jnp.dot(actsh[i], tile, preferred_element_type=F32)
        base[j] = total

        @pl.when(j + 3 < n_chunk)
        def _():
            start(down_copies(slot, j + 3))

        @pl.when(j >= 1)
        def _():
            send_sum(j - 1)

    send_sum(n_chunk - 1)

    @pl.loop(0, n_chunk)
    def _(j):
        for c in first_stage(j):
            c.wait_recv()
        passed = 2 - j % 2
        acc[j, passed] = acc[j, passed] + r1[j, 1]
        second_stage(j).start()
        base[j] = base[j] + (acc[j, 0] + r1[j, 0])

    @pl.loop(0, n_chunk)
    def _(j):
        second_stage(j).wait_recv()
        cols = pl.ds(pl.multiple_of(j * CHUNK, CHUNK), CHUNK)
        out_ref[:, cols] = (base[j] + r2[j]).astype(BF16)

    for c in rw_copies + [to_mate, x_a, x_b, y_a, y_b, d_a, d_b, m_x, m_y, m_d]:
        c.wait_send()
    swap(n_chunk - 2).wait_send()
    swap(n_chunk - 1).wait_send()

    @pl.loop(0, n_chunk)
    def _(j):
        for c in first_stage(j):
            c.wait_send()
        second_stage(j).wait_send()


def moe(h, table, resid, eg, eu, ed, sg, su, sd):
    rows, d_model = h.shape
    n_exp, _, ff = eg.shape
    n_chunk = d_model // CHUNK
    slots = 8 * CAP
    vmem = pl.BlockSpec(memory_space=pltpu.VMEM)
    hbm = pl.BlockSpec(memory_space=pl.ANY)
    dma = pltpu.SemaphoreType.DMA
    scratch = [
        pltpu.VMEM((3, 2, d_model, ff), BF16),
        pltpu.VMEM((4, 2 * rows, d_model), BF16),
        pltpu.VMEM((n_exp, slots, d_model), BF16),
        pltpu.VMEM((slots, ff), BF16),
        pltpu.VMEM((2, rows, ff), BF16),
        pltpu.VMEM((n_chunk, 4, rows, CHUNK), F32),
        pltpu.VMEM((n_chunk, 4, rows, CHUNK), F32),
        pltpu.VMEM((n_chunk, 2, rows, CHUNK), F32),
        pltpu.VMEM((n_chunk, rows, CHUNK), F32),
        pltpu.VMEM((2, 4, rows, CHUNK), F32),
        pltpu.VMEM((n_chunk, rows, CHUNK), F32),
        pltpu.VMEM((4, 3, 2 * rows, n_exp * 2 * CAP), BF16),
        pltpu.VMEM((n_exp * 2 * CAP, 2 * rows), F32),
        pltpu.VMEM((n_exp * 2 * CAP, 2 * rows), BF16),
        pltpu.VMEM((4, n_exp * 2 * CAP, CHUNK), BF16),
        pltpu.VMEM((4, 2, n_exp, rows), F32),
        dma((3, 10)), dma((10,)), dma((10,)), dma((7,)), dma((7,)), dma((n_chunk,)), dma((n_chunk,)),
        dma((n_chunk, 2)), dma((n_chunk, 2)), dma((n_chunk,)), dma((n_chunk,)),
    ]
    return pl.pallas_call(
        moe_kernel,
        out_shape=jax.ShapeDtypeStruct((rows, d_model), BF16),
        in_specs=[vmem] * 3 + [hbm] * 6,
        out_specs=vmem,
        scratch_shapes=scratch,
        compiler_params=pltpu.CompilerParams(collective_id=0, has_side_effects=True, vmem_limit_bytes=67043328),
        cost_estimate=pl.CostEstimate(flops=40_000_000_000, bytes_accessed=175_000_000, transcendentals=0),
    )(h, table, resid, eg, eu, ed, sg, su, sd)


def solution(mesh):
    row_one = P(('dp', 'ep'))
    row_two = P(('dp', 'ep'), None)
    row_three = P(('dp', 'ep'), None, None)
    rep_one = P(None)
    rep_two = P(None, None)
    rep_three = P(None, None, None)
    exp_spec = P('ep', None, None)

    def local_step(tok_in, lat_cache, rope_cache, tok_pos, expert_ids, attn_gain, w_query, w_kvdown, w_ukey, w_uval, w_out, ffn_gain, w_router, sh_gate, sh_up, sh_down, ex_gate, ex_up, ex_down):
        resid_bf, h_norm, lat_out, rope_out = attention_block(tok_in, lat_cache, rope_cache, tok_pos, attn_gain, w_query, w_kvdown, w_ukey, w_uval, w_out, ffn_gain)
        table = route_table(h_norm, w_router, expert_ids)
        out_hidden = moe(h_norm, table, resid_bf, ex_gate, ex_up, ex_down, sh_gate, sh_up, sh_down)
        return out_hidden, lat_out, rope_out

    in_specs = (row_two, row_three, row_three, row_one, row_two, rep_one, rep_two, rep_two, rep_three, rep_three, rep_two, rep_one, rep_two, rep_two, rep_two, rep_two, exp_spec, exp_spec, exp_spec)
    out_specs = (row_two, row_three, row_three)
    return jax.shard_map(local_step, mesh=mesh, in_specs=in_specs, out_specs=out_specs, check_vma=False)
```

time: 328 us -> 179 us (0.55); the launches traced: 324 us -> 179 us
  Pallas kernels: 0 us -> 98.8 us
  matrix products: 143 us -> 44.6 us
  blocking collectives: 75.8 us -> 0 us
  waiting for transfers between devices: 63.8 us -> 0 us
  starting transfers between devices: 3.6 us -> 0 us
    pallas_call x0 -> x1, Pallas kernels: none -> 98.8 us  [moe(): pl.pallas_call(moe_kernel, out_shape=jax.ShapeDtypeStruct((rows, d_model)...]
    dot_general x8 -> x1, matrix products: 97.5 us -> 0.34 us  [route_table(): jnp.dot(h_norm, w_router, preferred_element_type=jnp.float32)]
    all_to_all x1 -> x0, blocking collectives: 75.8 us -> none  [local_step(): recv_rows = lax.all_to_all(send_rows, 'ep', 0, 2, tiled=True)]
    all_to_all x1 -> x0, waiting for transfers between devices: 63.8 us -> none  [local_step(): back_rows = lax.all_to_all(exp_out, 'ep', 2, 0, tiled=True)]
    unnamed x15 -> x24, local copies, waits for them, and re-layouts: 0.49 us -> 7 us
    reshape x1 -> x0, local copies, waits for them, and re-layouts: 6.1 us -> none  [local_step(): exp_out = exp_out.reshape(1, local_experts, ep_size * cap_slots, d_model)]
    all_to_all x1 -> x0, starting transfers between devices: 3.6 us -> none  [local_step(): back_rows = lax.all_to_all(exp_out, 'ep', 2, 0, tiled=True)]
  transfers between devices with their start and end apart: 1 -> 0, of which waited for: 1 -> 0; matrix products, arithmetic and copies ran while one was open for 2% -> 0% of each run, Pallas kernels for 0% -> 0%
where the time goes in v1:
time: 179 us
  Pallas kernels  98.8 us (55%)
  matrix products  44.6 us (25%)
  other arithmetic  26.2 us (15%)
  local copies, waits for them, and re-layouts  8.42 us (5%)
    pallas_call x1, Pallas kernels, moe(): pl.pallas_call(moe_kernel, out_shape=jax.ShapeDtypeStruct((rows, d_model)...  98.8 us
    select_n x1, other arithmetic, attention_block(): lat_out = jnp.where(at_pos, lat_new[:, None, :], lat_cache)  14.5 us
    dot_general x1, matrix products, attention_block(): jnp.einsum('bhs,bsc->bhc', prob_mat, lat_out, preferred_element_type=jnp....  13.9 us
    dot_general x1, matrix products, attention_block(): jnp.einsum('bhc,bsc->bhs', q_lat, lat_out, preferred_element_type=jnp.flo...  9.55 us
    unnamed x24, local copies, waits for them, and re-layouts  7 us
    dot_general x1, matrix products, attention_block(): jnp.dot(x_norm, w_query, preferred_element_type=jnp.float32)  6.49 us
    dot_general x1, matrix products, attention_block(): jnp.dot(o_heads.reshape(tok_rows, -1), w_out, preferred_element_type=jnp....  4.8 us
    dot_general x1, matrix products, attention_block(): jnp.einsum('bhc,hcv->bhv', o_lat, w_uval, preferred_element_type=jnp.floa...  4.26 us

profile of v1, /device:TPU:0, one launch (start us, length us, event | category | flops | bytes accessed | tf_op | source)
XLA Modules:
  0.0 178.9 jit_solution(385670629221459862)
XLA Ops:
  0.6 0.7 convert_element_type.72
  1.3 1.2 fusion.27
  2.5 0.0 copy-start
  2.5 0.7 convert_element_type.65
  3.3 1.3 fusion.36
  4.6 1.3 convert_element_type.80
  5.9 1.3 iota_compare_fusion.2
  7.2 2.7 %fusion.37 = f32[128,576]{0,1:T(8,128)S(1)} fusion(bf16[2048,576]{0,1:T(8,128)(2,1)} %param.26, bf16[128,2048]{1,0:T(8,128)(2,1)} %param.19, f32[2048]{0:T(1024)S(1)} %convert_element_type.65, f32[128]{0:T(128)S(1)} %add_rsqrt_fusion.2), kind=kOutput, calls=%fused_computation.46 | convolution fusion | flops 303038464 | bytes 3187200 | tf_op jit(solution)/shard_map/dot_general | solution.py:45
  9.9 0.1 multiply_reduce_fusion
  10.0 0.1 multiply_cosine_fusion
  10.2 0.1 copy.38
  10.3 0.7 copy.43
  11.1 0.1 copy.41
  11.1 0.1 copy.42
  11.2 0.0 copy-done
  11.3 6.5 %convolution_convert_fusion = bf16[128,3072]{1,0:T(8,128)(2,1)S(1)} fusion(bf16[2048,3072]{1,0:T(8,128)(2,1)} %param.25, bf16[128,2048]{1,0:T(8,128)(2,1)S(1)} %copy-done, f32[2048]{0:T(1024)S(1)} %convert_element_type.65, f32[128]{0:T(128)S(1)} %add_rsqrt_fusion.2), kind=kOutput, calls=%fused_computation.2 | convolution fusion | flops 1612054528 | bytes 13902336 | tf_op jit(solution)/shard_map/dot_general | solution.py:44
  17.8 0.4 copy.36
  18.2 0.4 copy.48
  18.6 0.0 copy-start.4
  18.6 0.1 convert_element_type.71
  18.7 0.5 subtract_convert_fusion
  19.2 1.0 copy-done.4
  20.2 0.0 copy-start.5
  20.2 0.0 copy-start.7
  20.2 0.8 convert_bitcast_fusion
  21.0 0.8 copy-done.5
  21.8 0.0 copy-done.7
  21.8 1.3 broadcast_select_fusion.1
  23.1 0.0 copy-start.1
  23.1 1.3 copy-done.1
  24.4 1.7 fusion.31
  26.2 0.0 copy-start.8
  26.2 14.5 %broadcast_select_fusion = bf16[128,128,512]{2,1,0:T(8,128)(2,1)} fusion(bf16[128,128,512]{2,1,0:T(8,128)(2,1)} %param.20, pred[128,128]{1,0:T(8,128)(4,1)S(1)} %get-tuple-element.12, bf16[128,512]{1,0:T(8,128)(2,1)S(1)} %copy.38), kind=kLoop, calls=%fused_computation.1 | loop fusion | flops 8388608 | bytes 33701888 | tf_op jit(solution)/shard_map/jit(_where)/select_n | solution.py:54
  40.7 0.0 copy-done.8
  40.7 9.6 %fusion.14 = f32[128,16,128]{2,1,0:T(8,128)} fusion(f32[128,16,128]{2,1,0:T(8,128)} %fusion.31, bf16[128,128,512]{2,1,0:T(8,128)(2,1)} %broadcast_select_fusion, bf16[128,16,512]{2,0,1:T(8,128)(2,1)S(1)} %convert_bitcast_fusion, pred[128,128]{1,0:T(8,128)(4,1)S(1)} %copy-done.8), kind=kOutput, calls=%fused_computation.18 | convolution fusion | flops 269221888 | bytes 20987904 | tf_op jit(solution)/shard_map/bhc,bsc->bhs/dot_general | solution.py:56
  50.2 2.2 %fusion.42 = f32[128,16]{1,0:T(8,128)S(1)} fusion(f32[128,16,128]{2,1,0:T(8,128)} %fusion.14), kind=kOutput, calls=%fused_computation.61 | output fusion | flops 524415 | bytes 1056768 | tf_op jit(solution)/shard_map/sub | solution.py:61
  52.4 13.9 %convolution_convert_fusion.1 = bf16[128,16,512]{2,1,0:T(8,128)(2,1)S(1)} fusion(bf16[128,128,512]{2,1,0:T(8,128)(2,1)} %broadcast_select_fusion, f32[128,16]{1,0:T(8,128)S(1)} %fusion.42, f32[128,16,128]{2,1,0:T(8,128)} %fusion.14), kind=kOutput, calls=%fused_computation.11 | convolution fusion | flops 270272640 | bytes 19931136 | tf_op jit(solution)/shard_map/bhs,bsc->bhc/dot_general | solution.py:62
  66.3 4.3 %fusion.17 = bf16[16,128,128]{1,2,0:T(8,128)(2,1)S(1)} fusion(bf16[16,512,128]{2,1,0:T(8,128)(2,1)} %param.28, bf16[128,16,512]{2,1,0:T(8,128)(2,1)S(1)} %convolution_convert_fusion.1), kind=kOutput, calls=%fused_computation.21 | convolution fusion | flops 268697600 | bytes 4718592 | tf_op jit(solution)/shard_map/bhc,hcv->bhv/dot_general | solution.py:63
  70.6 0.0 copy-start.10
  70.6 0.0 copy-start.6
  70.6 0.0 copy-start.9
  70.6 4.8 %fusion.24 = (f32[128]{0:T(128)S(1)}, bf16[128,2048]{1,0:T(8,128)(2,1)S(1)}) fusion(bf16[128,2048]{0,1:T(8,128)(2,1)S(1)} %bitcast.23, bf16[2048,2048]{1,0:T(8,128)(2,1)} %param.29, bf16[128,2048]{1,0:T(8,128)(2,1)S(1)} %copy-done), kind=kOutput, calls=%fused_computation.27 | convolution fusion | flops 1075314560 | bytes 9961984 | tf_op jit(solution)/shard_map/dot_general | solution.py:64
  75.4 0.0 copy-start.2
  75.5 0.8 copy-done.2
  76.2 0.0 copy-done.10
  76.2 0.2 fusion.26.h_ref
  76.4 0.0 copy-start.3
  76.5 0.8 copy-done.3
  77.2 0.0 copy-done.6
  77.2 0.0 copy-done.9
  77.2 0.3 fusion.43
  77.6 0.6 divide_bitcast_fusion.rw_ref
  78.2 98.8 %shard_map.202 = bf16[128,2048]{1,0:T(8,128)(2,1)} custom-call(bf16[128,2048]{1,0:T(8,128)(2,1)} %copy-done.3, f32[64,128]{1,0:T(8,128)} %divide_bitcast_fusion.rw_ref, bf16[128,2048]{1,0:T(8,128)(2,1)} %copy-done.2, bf16[8,2048,1408]{2,1,0:T(8,128)(2,1)} %eg.1, bf16[8,2048,1408]{2,1,0:T(8,128)(2,1)} %eu.1, bf16[8,1408,2048]{2,1,0:T(8,128)(2,1)} %ed.1, ...), custom_call_target="tpu_custom_call" | custom-call | flops 40000000000 | bytes 175000000 | tf_op jit(solution)/shard_map/pallas_call | solution.py:356
  177.0 1.9 %copy.62 = bf16[128,2048]{1,0:T(8,128)(2,1)} copy(bf16[128,2048]{1,0:T(8,128)(2,1)} %shard_map.202) | data formatting | bytes 1048576
  (7 shorter events, 0.1 us)
Async XLA Ops:
  2.5 8.7 %copy-start = (bf16[128,2048]{1,0:T(8,128)(2,1)S(1)}, bf16[128,2048]{1,0:T(8,128)(2,1)}, u32[]{:S(2)}) copy-start(bf16[128,2048]{1,0:T(8,128)(2,1)} %param.19) | copy-start | bytes 1572868
  18.6 1.6 copy-start.4
  20.2 1.6 copy-start.5
  20.2 1.6 copy-start.7
  23.1 1.3 copy-start.1
  26.2 14.5 %copy-start.8 = (pred[128,128]{1,0:T(8,128)(4,1)S(1)}, pred[128,128]{1,0:T(8,128)(4,1)}, u32[]{:S(2)}) copy-start(pred[128,128]{1,0:T(8,128)(4,1)} %get-tuple-element.11) | copy-start | bytes 49156
  70.6 5.6 %copy-start.10 = (f32[2048]{0:T(1024)S(1)}, f32[2048]{0:T(1024)}, u32[]{:S(2)}) copy-start(f32[2048]{0:T(1024)} %convert_element_type.80) | copy-start | bytes 24580
  70.6 6.6 %copy-start.6 = (bf16[2048,64]{0,1:T(8,128)(2,1)S(1)}, bf16[2048,64]{0,1:T(8,128)(2,1)}, u32[]{:S(2)}) copy-start(bf16[2048,64]{0,1:T(8,128)(2,1)} %param.31) | copy-start | bytes 786436
  70.6 6.6 %copy-start.9 = (pred[128,64]{0,1:T(8,128)(4,1)S(1)}, pred[128,64]{0,1:T(8,128)(4,1)}, u32[]{:S(2)}) copy-start(pred[128,64]{0,1:T(8,128)(4,1)} %fusion.36) | copy-start | bytes 24580
  75.4 0.8 copy-start.2
  76.4 0.8 copy-start.3

commit v2 on v1

--- a/solution.py
+++ b/solution.py
@@ -1,5 +1,3 @@
-import functools
-
 import jax
 import jax.numpy as jnp
 from jax import lax
@@ -12,68 +10,207 @@
 NORM_EPS = 1e-6
 CAP = 24
 CHUNK = 256
+BLK = 16
 F32 = jnp.float32
 BF16 = jnp.bfloat16
 
 
-def unit_norm(values):
-    mean_sq = jnp.mean(jnp.square(values), axis=-1, keepdims=True)
-    return values * lax.rsqrt(mean_sq + NORM_EPS)
-
-
-def rms_norm(values, gain_vec):
-    return unit_norm(values) * gain_vec.astype(jnp.float32)
-
-
-def rope_rotate(values, angle_rad):
-    half_dim = values.shape[-1] // 2
-    x_first = values[..., :half_dim]
-    x_second = values[..., half_dim:]
-    cos_part = jnp.cos(angle_rad)
-    sin_part = jnp.sin(angle_rad)
-    return jnp.concatenate([x_first * cos_part - x_second * sin_part, x_second * cos_part + x_first * sin_part], axis=-1)
-
-
-def attention_block(tok_in, lat_cache, rope_cache, tok_pos, attn_gain, w_query, w_kvdown, w_ukey, w_uval, w_out, ffn_gain):
-    num_heads, nope_dim, kv_rank = w_ukey.shape
-    rope_dim = rope_cache.shape[-1]
-    seq_len = lat_cache.shape[1]
-    tok_rows = tok_in.shape[0]
-    x_wide = tok_in.astype(jnp.float32)
-    x_norm = rms_norm(x_wide, attn_gain).astype(jnp.bfloat16)
-    q_all = jnp.dot(x_norm, w_query, preferred_element_type=jnp.float32).astype(jnp.bfloat16).reshape(tok_rows, num_heads, nope_dim + rope_dim)
-    kv_all = jnp.dot(x_norm, w_kvdown, preferred_element_type=jnp.float32)
-    inv_freq = ROPE_BASE ** (-(2.0 * jnp.arange(rope_dim // 2)) / rope_dim)
-    angle_rad = tok_pos.astype(jnp.float32)[:, None] * inv_freq[None, :]
-    lat_new = unit_norm(kv_all[:, :kv_rank]).astype(jnp.bfloat16)
-    rope_new = rope_rotate(kv_all[:, kv_rank:], angle_rad).astype(jnp.bfloat16)
-    q_rope = rope_rotate(q_all[:, :, nope_dim:].astype(jnp.float32), angle_rad[:, None, :]).astype(jnp.bfloat16)
-    q_lat = jnp.einsum('bhn,hnc->bhc', q_all[:, :, :nope_dim], w_ukey, preferred_element_type=jnp.float32).astype(jnp.bfloat16)
-    seq_ids = jnp.arange(seq_len)
-    at_pos = (seq_ids[None, :] == tok_pos[:, None])[:, :, None]
-    lat_out = jnp.where(at_pos, lat_new[:, None, :], lat_cache)
-    rope_out = jnp.where(at_pos, rope_new[:, None, :], rope_cache)
-    scores = jnp.einsum('bhc,bsc->bhs', q_lat, lat_out, preferred_element_type=jnp.float32)
-    scores = scores + jnp.einsum('bhr,bsr->bhs', q_rope, rope_out, preferred_element_type=jnp.float32)
-    scores = scores * (nope_dim + rope_dim) ** -0.5
-    visible = (seq_ids[None, :] <= tok_pos[:, None])[:, None, :]
-    scores = jnp.where(visible, scores, -jnp.inf)
-    prob_mat = jax.nn.softmax(scores, axis=-1).astype(jnp.bfloat16)
-    o_lat = jnp.einsum('bhs,bsc->bhc', prob_mat, lat_out, preferred_element_type=jnp.float32).astype(jnp.bfloat16)
-    o_heads = jnp.einsum('bhc,hcv->bhv', o_lat, w_uval, preferred_element_type=jnp.float32).astype(jnp.bfloat16)
-    attn_out = jnp.dot(o_heads.reshape(tok_rows, -1), w_out, preferred_element_type=jnp.float32)
-    resid_bf = (x_wide + attn_out).astype(jnp.bfloat16)
-    h_norm = rms_norm(resid_bf.astype(jnp.float32), ffn_gain).astype(jnp.bfloat16)
-    return resid_bf, h_norm, lat_out, rope_out
-
-
-def route_table(h_norm, w_router, expert_ids):
-    num_experts = w_router.shape[1]
-    gate_prob = jax.nn.sigmoid(jnp.dot(h_norm, w_router, preferred_element_type=jnp.float32))
-    picked = jnp.any(expert_ids[:, :, None] == jnp.arange(num_experts)[None, None, :], axis=1)
-    chosen = jnp.where(picked, gate_prob, 0.0)
-    table = ROUTE_SCALE * chosen / jnp.sum(chosen, axis=1, keepdims=True)
-    return table.T
+def attn_kernel(pos_ref, x_ref, gain_ref, cos_ref, sin_ref, ids_ref, fgain_ref, wkv, wq, wuk, wuv, wo, wr, lat_in, rope_in,
+                lat_out, rope_out, res_ref, h_ref, rw_ref,
+                vkv, vq, vuk, vuv, vo, vr, lat, rop, xn, qlat, qrope, latn, ropen, olat, ohd, w_sem, lat_sem, rope_sem, lo_sem, ro_sem):
+    rows, d_model = x_ref.shape
+    n_head, nope, rank = wuk.shape
+    rdim = rope_in.shape[1]
+    seq = lat_in.shape[1]
+    qk = nope + rdim
+    n_blk = rows // BLK
+    scale = qk ** -0.5
+    pair = 2 * qk
+    n_pair = n_head // 2
+
+    def q_copy(m):
+        cols = slice(m * pair, (m + 1) * pair)
+        return pltpu.make_async_copy(wq.at[:, cols], vq.at[:, cols], w_sem.at[m])
+
+    kv_copy = pltpu.make_async_copy(wkv, vkv, w_sem.at[n_pair])
+    uk_copy = pltpu.make_async_copy(wuk, vuk, w_sem.at[n_pair + 1])
+    uv_copy = pltpu.make_async_copy(wuv, vuv, w_sem.at[n_pair + 2])
+    o_copy = pltpu.make_async_copy(wo, vo, w_sem.at[n_pair + 3])
+    r_copy = pltpu.make_async_copy(wr, vr, w_sem.at[n_pair + 4])
+
+    def lat_load(b):
+        return pltpu.make_async_copy(lat_in.at[pl.ds(b * BLK, BLK)], lat.at[pl.ds(b * BLK, BLK)], lat_sem.at[b])
+
+    def rope_load(b):
+        return pltpu.make_async_copy(rope_in.at[pl.ds(b * BLK, BLK)], rop.at[pl.ds(b * BLK, BLK)], rope_sem.at[b])
+
+    def lat_save(b):
+        return pltpu.make_async_copy(lat.at[pl.ds(b * BLK, BLK)], lat_out.at[pl.ds(b * BLK, BLK)], lo_sem.at[b])
+
+    def rope_save(b):
+        return pltpu.make_async_copy(rop.at[pl.ds(b * BLK, BLK)], rope_out.at[pl.ds(b * BLK, BLK)], ro_sem.at[b])
+
+    kv_copy.start()
+    for m in range(n_pair):
+        q_copy(m).start()
+        if m == 0:
+            uk_copy.start()
+
+    @pl.loop(0, n_blk)
+    def _(b):
+        lat_load(b).start()
+        rope_load(b).start()
+
+    uv_copy.start()
+    o_copy.start()
+    r_copy.start()
+
+    xw = x_ref[...].astype(F32)
+    xn[...] = (xw * lax.rsqrt(jnp.mean(xw * xw, axis=-1, keepdims=True) + NORM_EPS) * gain_ref[...].astype(F32)).astype(BF16)
+    lane = lax.broadcasted_iota(jnp.int32, (rows, 2 * rdim), 1)
+    front = lane % rdim < rdim // 2
+    low = lane < rdim
+    cos_t = cos_ref[...]
+    sin_t = sin_ref[...]
+
+    def rotate(v):
+        swapped = jnp.where(front, pltpu.roll(v, 2 * rdim - rdim // 2, 1), pltpu.roll(v, rdim // 2, 1))
+        return v * cos_t + swapped * sin_t
+
+    kv_copy.wait()
+    kv = lax.dot_general(xn[...], vkv[...], (((1,), (1,)), ((), ())), preferred_element_type=F32)
+    lat_raw = kv[:, 0:rank]
+    latn[...] = (lat_raw * lax.rsqrt(jnp.mean(lat_raw * lat_raw, axis=-1, keepdims=True) + NORM_EPS)).astype(BF16).astype(F32)
+    kr = kv[:, rank:rank + rdim]
+    ropen[...] = rotate(jnp.concatenate([kr, kr], axis=1)).astype(BF16).astype(F32)
+
+    for m in range(n_pair):
+        q_copy(m).wait()
+        if m == 0:
+            uk_copy.wait()
+        qf = jnp.dot(xn[...], vq[:, m * pair:(m + 1) * pair], preferred_element_type=F32).astype(BF16).astype(F32)
+        qa, qb, qc = qf[:, 0:nope], qf[:, nope:2 * nope], qf[:, 2 * nope:3 * nope]
+        second = pltpu.roll(jnp.where(low, qc, qb), rdim, 1)
+        turned = rotate(jnp.where(low, qb, qc))
+        qrope[2 * m] = turned[:, 0:rdim].astype(BF16)
+        qrope[2 * m + 1] = pltpu.roll(turned, rdim, 1)[:, 0:rdim].astype(BF16)
+        qlat[2 * m] = jnp.dot(qa.astype(BF16), vuk[2 * m], preferred_element_type=F32).astype(BF16)
+        qlat[2 * m + 1] = jnp.dot(second.astype(BF16), vuk[2 * m + 1], preferred_element_type=F32).astype(BF16)
+
+    grp = BLK * n_head
+    row_i = lax.broadcasted_iota(jnp.int32, (grp, grp), 0)
+    col_i = lax.broadcasted_iota(jnp.int32, (grp, grp), 1)
+    perm = jnp.where(col_i == (row_i % n_head) * BLK + row_i // n_head, 1.0, 0.0).astype(BF16)
+
+    @pl.loop(0, n_blk)
+    def _(b):
+        t0 = pl.multiple_of(b * BLK, BLK)
+        lat_load(b).wait()
+        rope_load(b).wait()
+        news = jnp.transpose(ropen[pl.ds(t0, BLK), :])
+        slane = lax.broadcasted_iota(jnp.int32, (rdim, seq), 1)
+        srow = lax.broadcasted_iota(jnp.int32, (16, rank), 0)
+        for t in range(BLK):
+            p = pos_ref[t0 + t]
+            lo = pl.multiple_of((p // 16) * 16, 16)
+            old = lat[t0 + t, pl.ds(lo, 16), :]
+            lat[t0 + t, pl.ds(lo, 16), :] = jnp.where(srow == p - lo, latn[pl.ds(t0 + t, 1), :], old.astype(F32)).astype(BF16)
+            rop[t0 + t] = jnp.where(slane == p, news[0:rdim, t:t + 1], rop[t0 + t].astype(F32)).astype(BF16)
+        q_blk = jnp.dot(perm, qlat[:, pl.ds(t0, BLK), :].reshape(grp, rank), preferred_element_type=F32).astype(BF16)
+        r_blk = jnp.dot(perm, qrope[:, pl.ds(t0, BLK), :].reshape(grp, rdim), preferred_element_type=F32).astype(BF16)
+        klane = lax.broadcasted_iota(jnp.int32, (n_head, seq), 1)
+        scores = []
+        for t in range(BLK):
+            s = lax.dot_general(q_blk[t * n_head:(t + 1) * n_head], lat[t0 + t], (((1,), (1,)), ((), ())), preferred_element_type=F32)
+            s = s + jnp.dot(r_blk[t * n_head:(t + 1) * n_head], rop[t0 + t], preferred_element_type=F32)
+            scores.append(jnp.where(klane <= pos_ref[t0 + t], s * scale, -jnp.inf))
+        sc = jnp.concatenate(scores, axis=0)
+        ex = jnp.exp(sc - jnp.max(sc, axis=-1, keepdims=True))
+        prob = (ex / jnp.sum(ex, axis=-1, keepdims=True)).astype(BF16)
+        outs = [jnp.dot(prob[t * n_head:(t + 1) * n_head], lat[t0 + t], preferred_element_type=F32).astype(BF16) for t in range(BLK)]
+        mixed = jnp.dot(perm, jnp.concatenate(outs, axis=0), preferred_element_type=F32).astype(BF16)
+        olat[:, pl.ds(t0, BLK), :] = mixed.reshape(n_head, BLK, rank)
+        lat_save(b).start()
+        rope_save(b).start()
+
+    uv_copy.wait()
+    for h in range(n_head):
+        ohd[:, h * nope:(h + 1) * nope] = jnp.dot(olat[h], vuv[h], preferred_element_type=F32).astype(BF16)
+    o_copy.wait()
+    total = jnp.zeros((rows, 1), F32)
+    wide = 512
+    for n in range(0, d_model, wide):
+        part = jnp.dot(ohd[...], vo[:, n:n + wide], preferred_element_type=F32)
+        res = (x_ref[:, n:n + wide].astype(F32) + part).astype(BF16)
+        res_ref[:, n:n + wide] = res
+        resf = res.astype(F32)
+        total = total + jnp.sum(resf * resf, axis=-1, keepdims=True)
+    inv = lax.rsqrt(total * (1.0 / d_model) + NORM_EPS)
+    for n in range(0, d_model, wide):
+        h_ref[:, n:n + wide] = (res_ref[:, n:n + wide].astype(F32) * inv * fgain_ref[:, n:n + wide].astype(F32)).astype(BF16)
+    r_copy.wait()
+    gate = jax.nn.sigmoid(lax.dot_general(vr[...], h_ref[...], (((1,), (1,)), ((), ())), preferred_element_type=F32))
+    want = lax.broadcasted_iota(jnp.int32, gate.shape, 0)
+    picked = want == ids_ref[0:1, :]
+    for k in range(1, ids_ref.shape[0]):
+        picked = picked | (want == ids_ref[k:k + 1, :])
+    chosen = jnp.where(picked, gate, 0.0)
+    rw_ref[...] = ROUTE_SCALE * chosen / jnp.sum(chosen, axis=0, keepdims=True)
+
+    @pl.loop(0, n_blk)
+    def _(b):
+        lat_save(b).wait()
+        rope_save(b).wait()
+
+
+def attention(tok_in, lat_cache, rope_cache, tok_pos, expert_ids, attn_gain, w_query, w_kvdown, w_ukey, w_uval, w_out, ffn_gain, w_router):
+    rows, d_model = tok_in.shape
+    n_head, nope, rank = w_ukey.shape
+    seq, rdim = rope_cache.shape[1], rope_cache.shape[2]
+    n_exp = w_router.shape[1]
+    inv_freq = ROPE_BASE ** (-(2.0 * jnp.arange(rdim // 2)) / rdim)
+    angle = tok_pos.astype(F32)[:, None] * jnp.tile(inv_freq, 4)[None, :]
+    sign = jnp.tile(jnp.where(jnp.arange(rdim) < rdim // 2, -1.0, 1.0), 2)[None, :]
+    vmem = pl.BlockSpec(memory_space=pltpu.VMEM)
+    smem = pl.BlockSpec(memory_space=pltpu.SMEM)
+    hbm = pl.BlockSpec(memory_space=pl.ANY)
+    dma = pltpu.SemaphoreType.DMA
+    n_blk = rows // BLK
+    scratch = [
+        pltpu.VMEM((rank + rdim, d_model), BF16),
+        pltpu.VMEM(w_query.shape, BF16),
+        pltpu.VMEM(w_ukey.shape, BF16),
+        pltpu.VMEM(w_uval.shape, BF16),
+        pltpu.VMEM(w_out.shape, BF16),
+        pltpu.VMEM((n_exp, d_model), BF16),
+        pltpu.VMEM(lat_cache.shape, BF16),
+        pltpu.VMEM((rows, rdim, seq), BF16),
+        pltpu.VMEM((rows, d_model), BF16),
+        pltpu.VMEM((n_head, rows, rank), BF16),
+        pltpu.VMEM((n_head, rows, rdim), BF16),
+        pltpu.VMEM((rows, rank), F32),
+        pltpu.VMEM((rows, 2 * rdim), F32),
+        pltpu.VMEM((n_head, rows, rank), BF16),
+        pltpu.VMEM((rows, n_head * nope), BF16),
+        dma((n_head // 2 + 5,)), dma((n_blk,)), dma((n_blk,)), dma((n_blk,)), dma((n_blk,)),
+    ]
+    lat_out, rope_out, resid, h, table = pl.pallas_call(
+        attn_kernel,
+        out_shape=(
+            jax.ShapeDtypeStruct(lat_cache.shape, BF16),
+            jax.ShapeDtypeStruct((rows, rdim, seq), BF16),
+            jax.ShapeDtypeStruct((rows, d_model), BF16),
+            jax.ShapeDtypeStruct((rows, d_model), BF16),
+            jax.ShapeDtypeStruct((n_exp, rows), F32),
+        ),
+        in_specs=[smem] + [vmem] * 6 + [hbm] * 8,
+        out_specs=(hbm, hbm, vmem, vmem, vmem),
+        scratch_shapes=scratch,
+        compiler_params=pltpu.CompilerParams(vmem_limit_bytes=64000000),
+        cost_estimate=pl.CostEstimate(flops=5_000_000_000, bytes_accessed=66_000_000, transcendentals=0),
+    )(tok_pos, tok_in, attn_gain[None, :], jnp.cos(angle), jnp.sin(angle) * sign, expert_ids.T, ffn_gain[None, :],
+      w_kvdown.T, w_query, w_ukey, w_uval, w_out, w_router.T, lat_cache, jnp.swapaxes(rope_cache, 1, 2))
+    return resid, h, table, lat_out, jnp.swapaxes(rope_out, 1, 2)
 
 
 def moe_kernel(h_ref, rw_ref, res_ref, eg, eu, ed, sg, su, sd, out_ref,
@@ -374,8 +511,7 @@
     exp_spec = P('ep', None, None)
 
     def local_step(tok_in, lat_cache, rope_cache, tok_pos, expert_ids, attn_gain, w_query, w_kvdown, w_ukey, w_uval, w_out, ffn_gain, w_router, sh_gate, sh_up, sh_down, ex_gate, ex_up, ex_down):
-        resid_bf, h_norm, lat_out, rope_out = attention_block(tok_in, lat_cache, rope_cache, tok_pos, attn_gain, w_query, w_kvdown, w_ukey, w_uval, w_out, ffn_gain)
-        table = route_table(h_norm, w_router, expert_ids)
+        resid_bf, h_norm, table, lat_out, rope_out = attention(tok_in, lat_cache, rope_cache, tok_pos, expert_ids, attn_gain, w_query, w_kvdown, w_ukey, w_uval, w_out, ffn_gain, w_router)
         out_hidden = moe(h_norm, table, resid_bf, ex_gate, ex_up, ex_down, sh_gate, sh_up, sh_down)
         return out_hidden, lat_out, rope_out
 

time: 179 us -> 131 us (0.73)
  matrix products: 44.6 us -> 0 us
  Pallas kernels: 98.8 us -> 124 us
  other arithmetic: 26.2 us -> 1.64 us
  local copies, waits for them, and re-layouts: 8.42 us -> 4.64 us
    dot_general x9 -> x0, matrix products: 44.6 us -> none  [the longest x1 13.9 us: attention_block(): jnp.einsum('bhs,bsc->bhc', prob_mat, lat_out, preferred_element_type=jnp....]
    pallas_call x0 -> x1, Pallas kernels: none -> 25.7 us  [attention(): pl.pallas_call(attn_kernel, out_shape=(jax.ShapeDtypeStruct(lat_cache.sha...]
    select_n x2 -> x1, other arithmetic: 15.8 us -> 0.01 us  [attention(): jnp.where(jnp.arange(rdim) < rdim // 2, -1.0, 1.0)]
    unnamed x24 -> x1, local copies, waits for them, and re-layouts: 7 us -> 1.88 us
    broadcast_in_dim x0 -> x2, local copies, waits for them, and re-layouts: none -> 2.58 us  [the longest x1 1.3 us: attention(): ffn_gain[None, :]]
    convert_element_type x6 -> x1, other arithmetic: 2.97 us -> 0.66 us  [attention(): angle = tok_pos.astype(F32)[:, None] * jnp.tile(inv_freq, 4)[None, :]]
    sub x1 -> x0, other arithmetic: 2.16 us -> none  [attention_block(): prob_mat = jax.nn.softmax(scores, axis=-1).astype(jnp.bfloat16)]
where the time goes in v2:
time: 131 us
  Pallas kernels  124 us (95%)
  local copies, waits for them, and re-layouts  4.64 us (4%)
  other arithmetic  1.64 us (1%)
    pallas_call x1, Pallas kernels, moe(): pl.pallas_call(moe_kernel, out_shape=jax.ShapeDtypeStruct((rows, d_model)...  98.6 us
    pallas_call x1, Pallas kernels, attention(): pl.pallas_call(attn_kernel, out_shape=(jax.ShapeDtypeStruct(lat_cache.sha...  25.7 us

profile of v2, /device:TPU:0, one launch (start us, length us, event | category | flops | bytes accessed | tf_op | source)
XLA Modules:
  0.0 131.2 jit_solution(16283576650948875771)
XLA Ops:
  0.6 0.7 convert_element_type.10
  1.3 0.1 mul.41
  1.4 0.1 mul.38
  1.5 1.3 broadcast_in_dim.15.gain_ref
  2.8 1.3 broadcast_in_dim.18.fgain_ref
  4.1 1.0 fusion
  5.0 25.7 %shard_map.202 = (bf16[128,128,512]{2,1,0:T(8,128)(2,1)}, bf16[128,64,128]{2,1,0:T(8,128)(2,1)}, bf16[128,2048]{1,0:T(8,128)(2,1)}, bf16[128,2048]{1,0:T(8,128)(2,1)}, f32[64,128]{1,0:T(8,128)}) custom-call(s32[128]{0:T(128)} %pos_ref.1, bf16[128,2048]{1,0:T(8,128)(2,1)} %x_ref.1, bf16[1,2048]{1,0:T(2,128)(2,1)} %broadcast_in_dim.15.gain_ref, ...), custom_call_target="tpu_custom_call" | custom-call | flops 5000000000 | bytes 66000000 | tf_op jit(solution)/shard_map/pallas_call | solution.py:197
  30.8 98.6 %shard_map.203 = bf16[128,2048]{1,0:T(8,128)(2,1)} custom-call(bf16[128,2048]{1,0:T(8,128)(2,1)} %get-tuple-element.8.h_ref, f32[64,128]{1,0:T(8,128)} %get-tuple-element.9.rw_ref, bf16[128,2048]{1,0:T(8,128)(2,1)} %get-tuple-element.10.res_ref, bf16[8,2048,1408]{2,1,0:T(8,128)(2,1)} %eg.1, bf16[8,2048,1408]{2,1,0:T(8,128)(2,1)} %eu.1, ...), custom_call_target="tpu_custom_call" | custom-call | flops 40000000000 | bytes 175000000 | tf_op jit(solution)/shard_map/pallas_call | solution.py:493
  129.3 1.9 %copy.23 = bf16[128,2048]{1,0:T(8,128)(2,1)} copy(bf16[128,2048]{1,0:T(8,128)(2,1)} %shard_map.203) | data formatting | bytes 1048576
  (4 shorter events, 0.0 us)

commit v3 on v2

--- a/solution.py
+++ b/solution.py
@@ -1,5 +1,6 @@
 import jax
 import jax.numpy as jnp
+import numpy as np
 from jax import lax
 from jax.experimental import pallas as pl
 from jax.experimental.pallas import tpu as pltpu
@@ -11,11 +12,12 @@
 CAP = 24
 CHUNK = 256
 BLK = 16
+LAG = 4
 F32 = jnp.float32
 BF16 = jnp.bfloat16
 
 
-def attn_kernel(pos_ref, x_ref, gain_ref, cos_ref, sin_ref, ids_ref, fgain_ref, wkv, wq, wuk, wuv, wo, wr, lat_in, rope_in,
+def attn_kernel(pos_ref, prow_ref, x_ref, gain_ref, ids_ref, fgain_ref, wkv, wq, wuk, wuv, wo, wr, lat_in, rope_in,
                 lat_out, rope_out, res_ref, h_ref, rw_ref,
                 vkv, vq, vuk, vuv, vo, vr, lat, rop, xn, qlat, qrope, latn, ropen, olat, ohd, w_sem, lat_sem, rope_sem, lo_sem, ro_sem):
     rows, d_model = x_ref.shape
@@ -66,12 +68,17 @@
     r_copy.start()
 
     xw = x_ref[...].astype(F32)
-    xn[...] = (xw * lax.rsqrt(jnp.mean(xw * xw, axis=-1, keepdims=True) + NORM_EPS) * gain_ref[...].astype(F32)).astype(BF16)
+    xn[...] = (xw * lax.rsqrt(jnp.mean(xw * xw, axis=-1, keepdims=True) + NORM_EPS) * gain_ref[...].reshape(1, d_model).astype(F32)).astype(BF16)
     lane = lax.broadcasted_iota(jnp.int32, (rows, 2 * rdim), 1)
     front = lane % rdim < rdim // 2
     low = lane < rdim
-    cos_t = cos_ref[...]
-    sin_t = sin_ref[...]
+    where_in = lane % (rdim // 2)
+    freq = jnp.zeros(lane.shape, F32)
+    for i in range(rdim // 2):
+        freq = jnp.where(where_in == i, np.float32(ROPE_BASE ** (-2.0 * i / rdim)), freq)
+    angle = jnp.transpose(jnp.broadcast_to(prow_ref[...].astype(F32), (rows, rows))) * freq
+    cos_t = jnp.cos(angle)
+    sin_t = jnp.where(front, -jnp.sin(angle), jnp.sin(angle))
 
     def rotate(v):
         swapped = jnp.where(front, pltpu.roll(v, 2 * rdim - rdim // 2, 1), pltpu.roll(v, rdim // 2, 1))
@@ -145,9 +152,10 @@
         res_ref[:, n:n + wide] = res
         resf = res.astype(F32)
         total = total + jnp.sum(resf * resf, axis=-1, keepdims=True)
+    fgain = fgain_ref[...].reshape(1, d_model).astype(F32)
     inv = lax.rsqrt(total * (1.0 / d_model) + NORM_EPS)
     for n in range(0, d_model, wide):
-        h_ref[:, n:n + wide] = (res_ref[:, n:n + wide].astype(F32) * inv * fgain_ref[:, n:n + wide].astype(F32)).astype(BF16)
+        h_ref[:, n:n + wide] = (res_ref[:, n:n + wide].astype(F32) * inv * fgain[:, n:n + wide]).astype(BF16)
     r_copy.wait()
     gate = jax.nn.sigmoid(lax.dot_general(vr[...], h_ref[...], (((1,), (1,)), ((), ())), preferred_element_type=F32))
     want = lax.broadcasted_iota(jnp.int32, gate.shape, 0)
@@ -168,9 +176,6 @@
     n_head, nope, rank = w_ukey.shape
     seq, rdim = rope_cache.shape[1], rope_cache.shape[2]
     n_exp = w_router.shape[1]
-    inv_freq = ROPE_BASE ** (-(2.0 * jnp.arange(rdim // 2)) / rdim)
-    angle = tok_pos.astype(F32)[:, None] * jnp.tile(inv_freq, 4)[None, :]
-    sign = jnp.tile(jnp.where(jnp.arange(rdim) < rdim // 2, -1.0, 1.0), 2)[None, :]
     vmem = pl.BlockSpec(memory_space=pltpu.VMEM)
     smem = pl.BlockSpec(memory_space=pltpu.SMEM)
     hbm = pl.BlockSpec(memory_space=pl.ANY)
@@ -203,19 +208,19 @@
             jax.ShapeDtypeStruct((rows, d_model), BF16),
             jax.ShapeDtypeStruct((n_exp, rows), F32),
         ),
-        in_specs=[smem] + [vmem] * 6 + [hbm] * 8,
+        in_specs=[smem] + [vmem] * 5 + [hbm] * 8,
         out_specs=(hbm, hbm, vmem, vmem, vmem),
         scratch_shapes=scratch,
         compiler_params=pltpu.CompilerParams(vmem_limit_bytes=64000000),
         cost_estimate=pl.CostEstimate(flops=5_000_000_000, bytes_accessed=66_000_000, transcendentals=0),
-    )(tok_pos, tok_in, attn_gain[None, :], jnp.cos(angle), jnp.sin(angle) * sign, expert_ids.T, ffn_gain[None, :],
+    )(tok_pos, tok_pos[None, :], tok_in, attn_gain, expert_ids.T, ffn_gain,
       w_kvdown.T, w_query, w_ukey, w_uval, w_out, w_router.T, lat_cache, jnp.swapaxes(rope_cache, 1, 2))
     return resid, h, table, lat_out, jnp.swapaxes(rope_out, 1, 2)
 
 
-def moe_kernel(h_ref, rw_ref, res_ref, eg, eu, ed, sg, su, sd, out_ref,
+def moe_kernel(h_ref, rw_ref, res_hbm, eg, eu, ed, sg, su, sd, out_ref,
                ring, hall, xbuf, actt, actsh, acc, drecv, r1, r2, stage, base, pw, pwf, pbuf, ebuf, rwin,
-               ring_sem, ag_s, ag_r, rw_s, rw_r, d_s, d_r, s1_s, s1_r, s2_s, s2_r):
+               ring_sem, res_sem, ag_s, ag_r, rw_s, rw_r, d_s, d_r, s1_s, s1_r, s2_s, s2_r):
     rows = h_ref.shape[0]
     half = rows // 2
     d_model = h_ref.shape[1]
@@ -270,13 +275,14 @@
         for c in copies:
             c.wait()
 
+    barrier = pltpu.get_barrier_semaphore()
+    for _, _, dev in others:
+        pl.semaphore_signal(barrier, inc=1, device_id={'ep': dev}, device_id_type=pl.DeviceIdType.MESH)
     start(shared_copies(0, 0))
     start(shared_copies(1, 1))
     start(expert_copies(2, 0))
-
-    barrier = pltpu.get_barrier_semaphore()
-    for _, _, dev in others:
-        pl.semaphore_signal(barrier, inc=1, device_id={'ep': dev}, device_id_type=pl.DeviceIdType.MESH)
+    res_copy = pltpu.make_async_copy(res_hbm, out_ref, res_sem)
+    res_copy.start()
     pl.semaphore_wait(barrier, len(others))
 
     part_a, part_b = pl.ds(0, half), pl.ds(half, half)
@@ -292,7 +298,8 @@
     d_b = remote(hall.at[2, part_b], hall.at[3, part_b], ag_s.at[6], ag_r.at[6], xn)
     m_x = remote(hall.at[1, own], hall.at[1, other], ag_s.at[7], ag_r.at[7], mate)
     m_y = remote(hall.at[2, own], hall.at[2, other], ag_s.at[8], ag_r.at[8], mate)
-    m_d = remote(hall.at[3, own], hall.at[3, other], ag_s.at[9], ag_r.at[9], mate)
+    m_da = remote(hall.at[3, part_a], hall.at[3, pl.ds(rows, half)], ag_s.at[9], ag_r.at[9], mate)
+    m_db = remote(hall.at[3, part_b], hall.at[3, pl.ds(rows + half, half)], ag_s.at[10], ag_r.at[10], mate)
     for c in (x_a, y_b, to_mate, x_b, y_a):
         c.start()
 
@@ -301,7 +308,7 @@
     for c in rw_copies:
         c.wait_recv()
 
-    def gather_rows(r):
+    def tables(r):
         both = jnp.concatenate([rwin[r, 0], rwin[r, 1]], axis=1)
         two = 2 * rows
         t_in = lax.broadcasted_iota(jnp.int32, (two, two), 0)
@@ -314,13 +321,8 @@
         want = lax.broadcasted_iota(jnp.int32, (grp, two), 0)
         for e in range(n_exp):
             hit = want == slot[e:e + 1, :]
-            pbuf[e * grp:(e + 1) * grp, :] = jnp.where(hit, 1.0, 0.0).astype(BF16)
+            pbuf[r, e * grp:(e + 1) * grp, :] = jnp.where(hit, 1.0, 0.0).astype(BF16)
             pwf[e * grp:(e + 1) * grp, :] = jnp.where(hit, both[e:e + 1, :], 0.0)
-        wide = 512
-        for n in range(0, d_model, wide):
-            got = jnp.dot(pbuf[...], hall[r, :, n:n + wide], preferred_element_type=F32).astype(BF16)
-            for e in range(n_exp):
-                xbuf[e, r * grp:(r + 1) * grp, n:n + wide] = got[e * grp:(e + 1) * grp, :]
         turned = pwf[...].T
         hi = turned.astype(BF16)
         rest = turned - hi.astype(F32)
@@ -329,6 +331,13 @@
         pw[r, 1] = mid
         pw[r, 2] = (rest - mid.astype(F32)).astype(BF16)
 
+    def gather_rows(r):
+        wide = 512
+        for n in range(0, d_model, wide):
+            got = jnp.dot(pbuf[r], hall[r, :, n:n + wide], preferred_element_type=F32).astype(BF16)
+            for e in range(n_exp):
+                xbuf[e, r * grp:(r + 1) * grp, n:n + wide] = got[e * grp:(e + 1) * grp, :]
+
     def shared_item(i):
         wait(shared_copies(i, i))
         for n, w in mids:
@@ -337,13 +346,15 @@
             actsh[i, :, n:n + w] = (jax.nn.silu(g) * u).astype(BF16)
         start(expert_copies(i, i + 1))
 
+    for r in range(4):
+        tables(r)
+    to_mate.wait_recv()
+    gather_rows(0)
     shared_item(0)
     x_a.wait_recv()
     d_a.start()
     y_b.wait_recv()
     d_b.start()
-    to_mate.wait_recv()
-    gather_rows(0)
     shared_item(1)
     x_b.wait_recv()
     m_x.start()
@@ -354,10 +365,13 @@
     m_y.wait_recv()
     gather_rows(2)
     d_a.wait_recv()
+    m_da.start()
     d_b.wait_recv()
-    m_d.start()
-    m_d.wait_recv()
+    m_db.start()
+    m_da.wait_recv()
+    m_db.wait_recv()
     gather_rows(3)
+    res_copy.wait()
 
     @pl.loop(0, n_exp)
     def _(e):
@@ -377,15 +391,17 @@
         def _():
             start(down_copies(slot, e + 3 - n_exp))
 
+    side = CHUNK // 2
+
     def first_stage(j):
-        odd = j % 2
-        dev = xn + odd * (yn - xn)
-        return [remote(acc.at[j, 1 + odd], r1.at[j, 0], s1_s.at[j, 0], s1_r.at[j, 0], dev), remote(acc.at[j, 3], r1.at[j, 1], s1_s.at[j, 1], s1_r.at[j, 1], dev)]
+        out = []
+        for f, dev in enumerate((xn, yn)):
+            for q, r in enumerate((1 + f, 3)):
+                out.append(remote(acc.at[j, f, r], r1.at[j, f, q], s1_s.at[j, 2 * f + q], s1_r.at[j, 2 * f + q], dev))
+        return out
 
     def second_stage(j):
-        odd = j % 2
-        dev = yn + odd * (xn - yn)
-        return remote(acc.at[j, 2 - odd], r2.at[j], s2_s.at[j], s2_r.at[j], dev)
+        return [remote(acc.at[j, f, 2 - f], r2.at[j, f], s2_s.at[j, f], s2_r.at[j, f], dev) for f, dev in enumerate((yn, xn))]
 
     def swap(j):
         return remote(stage.at[j % 2], drecv.at[j], d_s.at[j], d_r.at[j], mate)
@@ -394,12 +410,24 @@
         swap(j).wait_recv()
         acc[j] = acc[j] + drecv[j]
         start(first_stage(j))
+
+    def pass_on(j):
+        for c in first_stage(j):
+            c.wait_recv()
+        for f, c in enumerate(second_stage(j)):
+            acc[j, f, 2 - f] = acc[j, f, 2 - f] + r1[j, f, 1]
+            c.start()
+        for f in range(2):
+            cut = slice(f * side, (f + 1) * side)
+            base[j, :, cut] = base[j, :, cut] + (acc[j, f, 0] + r1[j, f, 0])
 
     @pl.loop(0, n_chunk)
     def _(j):
         slot = (j + n_exp + 2) % 3
         wait(down_copies(slot, j))
         for e in range(n_exp):
+            if e == n_exp // 2:
+                pl.when(j >= 2)(lambda: send_sum(j - 1))
             tile = ring[slot, e // 5, 0:ff, (e % 5) * CHUNK:(e % 5 + 1) * CHUNK]
             got = jnp.dot(xbuf[e, :, 0:ff], tile, preferred_element_type=F32).astype(BF16)
             for r in range(4):
@@ -413,12 +441,14 @@
             part = jnp.dot(pw[r, 0], ebuf[r], preferred_element_type=F32)
             part = part + jnp.dot(pw[r, 1], ebuf[r], preferred_element_type=F32)
             part = part + jnp.dot(pw[r, 2], ebuf[r], preferred_element_type=F32)
-            acc[j, r] = part[0:rows, :]
-            stage[j % 2, r] = part[rows:, :]
+            for f in range(2):
+                cut = slice(f * side, (f + 1) * side)
+                acc[j, f, r] = part[0:rows, cut]
+                stage[j % 2, f, r] = part[rows:, cut]
         swap(j).start()
 
         cols = pl.ds(pl.multiple_of(j * CHUNK, CHUNK), CHUNK)
-        total = res_ref[:, cols].astype(F32)
+        total = out_ref[:, cols].astype(F32)
         for i in range(2):
             k = n_exp + i
             tile = ring[slot, k // 5, 0:ff, (k % 5) * CHUNK:(k % 5 + 1) * CHUNK]
@@ -429,37 +459,34 @@
         def _():
             start(down_copies(slot, j + 3))
 
-        @pl.when(j >= 1)
+        pl.when(j == 0)(lambda: send_sum(0))
+
+        @pl.when(j >= LAG)
         def _():
-            send_sum(j - 1)
+            pass_on(j - LAG)
 
     send_sum(n_chunk - 1)
+
+    @pl.loop(n_chunk - LAG, n_chunk)
+    def _(j):
+        pass_on(j)
 
     @pl.loop(0, n_chunk)
     def _(j):
-        for c in first_stage(j):
+        for f, c in enumerate(second_stage(j)):
             c.wait_recv()
-        passed = 2 - j % 2
-        acc[j, passed] = acc[j, passed] + r1[j, 1]
-        second_stage(j).start()
-        base[j] = base[j] + (acc[j, 0] + r1[j, 0])
-
-    @pl.loop(0, n_chunk)
-    def _(j):
-        second_stage(j).wait_recv()
-        cols = pl.ds(pl.multiple_of(j * CHUNK, CHUNK), CHUNK)
-        out_ref[:, cols] = (base[j] + r2[j]).astype(BF16)
-
-    for c in rw_copies + [to_mate, x_a, x_b, y_a, y_b, d_a, d_b, m_x, m_y, m_d]:
+            cut = slice(f * side, (f + 1) * side)
+            out_ref[:, pl.ds(pl.multiple_of(j * CHUNK + f * side, side), side)] = (base[j, :, cut] + r2[j, f]).astype(BF16)
+
+    for c in rw_copies + [to_mate, x_a, x_b, y_a, y_b, d_a, d_b, m_x, m_y, m_da, m_db]:
         c.wait_send()
     swap(n_chunk - 2).wait_send()
     swap(n_chunk - 1).wait_send()
 
     @pl.loop(0, n_chunk)
     def _(j):
-        for c in first_stage(j):
+        for c in first_stage(j) + second_stage(j):
             c.wait_send()
-        second_stage(j).wait_send()
 
 
 def moe(h, table, resid, eg, eu, ed, sg, su, sd):
@@ -476,24 +503,24 @@
         pltpu.VMEM((n_exp, slots, d_model), BF16),
         pltpu.VMEM((slots, ff), BF16),
         pltpu.VMEM((2, rows, ff), BF16),
-        pltpu.VMEM((n_chunk, 4, rows, CHUNK), F32),
-        pltpu.VMEM((n_chunk, 4, rows, CHUNK), F32),
-        pltpu.VMEM((n_chunk, 2, rows, CHUNK), F32),
-        pltpu.VMEM((n_chunk, rows, CHUNK), F32),
-        pltpu.VMEM((2, 4, rows, CHUNK), F32),
+        pltpu.VMEM((n_chunk, 2, 4, rows, CHUNK // 2), F32),
+        pltpu.VMEM((n_chunk, 2, 4, rows, CHUNK // 2), F32),
+        pltpu.VMEM((n_chunk, 2, 2, rows, CHUNK // 2), F32),
+        pltpu.VMEM((n_chunk, 2, rows, CHUNK // 2), F32),
+        pltpu.VMEM((2, 2, 4, rows, CHUNK // 2), F32),
         pltpu.VMEM((n_chunk, rows, CHUNK), F32),
         pltpu.VMEM((4, 3, 2 * rows, n_exp * 2 * CAP), BF16),
         pltpu.VMEM((n_exp * 2 * CAP, 2 * rows), F32),
-        pltpu.VMEM((n_exp * 2 * CAP, 2 * rows), BF16),
+        pltpu.VMEM((4, n_exp * 2 * CAP, 2 * rows), BF16),
         pltpu.VMEM((4, n_exp * 2 * CAP, CHUNK), BF16),
         pltpu.VMEM((4, 2, n_exp, rows), F32),
-        dma((3, 10)), dma((10,)), dma((10,)), dma((7,)), dma((7,)), dma((n_chunk,)), dma((n_chunk,)),
-        dma((n_chunk, 2)), dma((n_chunk, 2)), dma((n_chunk,)), dma((n_chunk,)),
+        dma((3, 10)), dma, dma((11,)), dma((11,)), dma((7,)), dma((7,)), dma((n_chunk,)), dma((n_chunk,)),
+        dma((n_chunk, 4)), dma((n_chunk, 4)), dma((n_chunk, 2)), dma((n_chunk, 2)),
     ]
     return pl.pallas_call(
         moe_kernel,
         out_shape=jax.ShapeDtypeStruct((rows, d_model), BF16),
-        in_specs=[vmem] * 3 + [hbm] * 6,
+        in_specs=[vmem] * 2 + [hbm] * 7,
         out_specs=vmem,
         scratch_shapes=scratch,
         compiler_params=pltpu.CompilerParams(collective_id=0, has_side_effects=True, vmem_limit_bytes=67043328),

time: 131 us -> 124 us (0.947)
  local copies, waits for them, and re-layouts: 4.64 us -> 1.88 us
  Pallas kernels: 124 us -> 122 us
  other arithmetic: 1.64 us -> 0 us
    pallas_call x1, Pallas kernels: 98.6 us -> 95.8 us  [moe(): pl.pallas_call(moe_kernel, out_shape=jax.ShapeDtypeStruct((rows, d_model)...]
    broadcast_in_dim x2 -> x0, local copies, waits for them, and re-layouts: 2.58 us -> none  [the longest x1 1.3 us: attention(): ffn_gain[None, :]]
where the time goes in v3:
time: 124 us
  Pallas kernels  122 us (98%)
  local copies, waits for them, and re-layouts  1.88 us (2%)
    pallas_call x1, Pallas kernels, moe(): pl.pallas_call(moe_kernel, out_shape=jax.ShapeDtypeStruct((rows, d_model)...  95.8 us
    pallas_call x1, Pallas kernels, attention(): pl.pallas_call(attn_kernel, out_shape=(jax.ShapeDtypeStruct(lat_cache.sha...  25.7 us

profile of v3, /device:TPU:0, one launch (start us, length us, event | category | flops | bytes accessed | tf_op | source)
XLA Modules:
  0.0 124.0 jit_solution(16354974710699657855)
XLA Ops:
  0.6 25.7 %shard_map.202 = (bf16[128,128,512]{2,1,0:T(8,128)(2,1)}, bf16[128,64,128]{2,1,0:T(8,128)(2,1)}, bf16[128,2048]{1,0:T(8,128)(2,1)}, bf16[128,2048]{1,0:T(8,128)(2,1)}, f32[64,128]{1,0:T(8,128)}) custom-call(s32[128]{0:T(128)} %pos_ref.1, s32[1,128]{1,0:T(1,128)} %bitcast.10, bf16[128,2048]{1,0:T(8,128)(2,1)} %x_ref.1, bf16[2048]{0:T(1024)(128)(2,1)} %gain_ref.1, ...), custom_call_target="tpu_custom_call" | custom-call | flops 5000000000 | bytes 66000000 | tf_op jit(solution)/shard_map/pallas_call | solution.py:202
  26.3 95.8 %shard_map.203 = bf16[128,2048]{1,0:T(8,128)(2,1)} custom-call(bf16[128,2048]{1,0:T(8,128)(2,1)} %get-tuple-element.8.h_ref, f32[64,128]{1,0:T(8,128)} %get-tuple-element.9.rw_ref, bf16[128,2048]{1,0:T(8,128)(2,1)} %get-tuple-element.10.res_hbm, bf16[8,2048,1408]{2,1,0:T(8,128)(2,1)} %eg.1, bf16[8,2048,1408]{2,1,0:T(8,128)(2,1)} %eu.1, ...), custom_call_target="tpu_custom_call" | custom-call | flops 40000000000 | bytes 175000000 | tf_op jit(solution)/shard_map/pallas_call | solution.py:520
  122.2 1.9 %copy.23 = bf16[128,2048]{1,0:T(8,128)(2,1)} copy(bf16[128,2048]{1,0:T(8,128)(2,1)} %shard_map.203) | data formatting | bytes 1048576

commit v4 on v3

--- a/solution.py
+++ b/solution.py
@@ -29,6 +29,7 @@
     scale = qk ** -0.5
     pair = 2 * qk
     n_pair = n_head // 2
+    deep = d_model // 2
 
     def q_copy(m):
         cols = slice(m * pair, (m + 1) * pair)
@@ -155,9 +156,10 @@
     fgain = fgain_ref[...].reshape(1, d_model).astype(F32)
     inv = lax.rsqrt(total * (1.0 / d_model) + NORM_EPS)
     for n in range(0, d_model, wide):
-        h_ref[:, n:n + wide] = (res_ref[:, n:n + wide].astype(F32) * inv * fgain[:, n:n + wide]).astype(BF16)
+        h_ref[n // deep, :, n % deep:n % deep + wide] = (res_ref[:, n:n + wide].astype(F32) * inv * fgain[:, n:n + wide]).astype(BF16)
     r_copy.wait()
-    gate = jax.nn.sigmoid(lax.dot_general(vr[...], h_ref[...], (((1,), (1,)), ((), ())), preferred_element_type=F32))
+    logits = [lax.dot_general(vr[:, k * deep:(k + 1) * deep], h_ref[k], (((1,), (1,)), ((), ())), preferred_element_type=F32) for k in range(2)]
+    gate = jax.nn.sigmoid(logits[0] + logits[1])
     want = lax.broadcasted_iota(jnp.int32, gate.shape, 0)
     picked = want == ids_ref[0:1, :]
     for k in range(1, ids_ref.shape[0]):
@@ -205,7 +207,7 @@
             jax.ShapeDtypeStruct(lat_cache.shape, BF16),
             jax.ShapeDtypeStruct((rows, rdim, seq), BF16),
             jax.ShapeDtypeStruct((rows, d_model), BF16),
-            jax.ShapeDtypeStruct((rows, d_model), BF16),
+            jax.ShapeDtypeStruct((2, rows, d_model // 2), BF16),
             jax.ShapeDtypeStruct((n_exp, rows), F32),
         ),
         in_specs=[smem] + [vmem] * 5 + [hbm] * 8,
@@ -218,16 +220,19 @@
     return resid, h, table, lat_out, jnp.swapaxes(rope_out, 1, 2)
 
 
-def moe_kernel(h_ref, rw_ref, res_hbm, eg, eu, ed, sg, su, sd, out_ref,
-               ring, hall, xbuf, actt, actsh, acc, drecv, r1, r2, stage, base, pw, pwf, pbuf, ebuf, rwin,
-               ring_sem, res_sem, ag_s, ag_r, rw_s, rw_r, d_s, d_r, s1_s, s1_r, s2_s, s2_r):
-    rows = h_ref.shape[0]
+def moe_kernel(h_hbm, rw_hbm, res_hbm, eg, eu, ed, sg, su, sd, out_ref,
+               ring, hall, xbuf, part, actsh, drecv, r1, r2, stage, pw, pwf, pbuf, rwin, rw_ref,
+               ring_sem, in_sem, ag_s, ag_r, rw_s, rw_r, d_s, d_r, s1_s, s1_r, s2_s, s2_r):
+    rows = rw_hbm.shape[1]
     half = rows // 2
-    d_model = h_ref.shape[1]
+    deep = h_hbm.shape[2]
+    d_model = 2 * deep
     ff = eg.shape[2]
     n_exp = eg.shape[0]
     n_chunk = d_model // CHUNK
+    side = CHUNK // 2
     grp = 2 * CAP
+    left = ff - deep
     mids = [(n, min(CHUNK, ff - n)) for n in range(0, ff, CHUNK)]
     me = lax.axis_index('ep')
     core = me % 2
@@ -242,31 +247,6 @@
     def remote(src, dst, ssem, rsem, dev):
         return pltpu.make_async_remote_copy(src_ref=src, dst_ref=dst, send_sem=ssem, recv_sem=rsem, device_id={'ep': dev}, device_id_type=pl.DeviceIdType.MESH)
 
-    step = d_model // 4
-
-    def pair_copies(slot, gate, up):
-        out = []
-        for b, src in enumerate((gate, up)):
-            for q in range(4):
-                out.append(pltpu.make_async_copy(src.at[pl.ds(q * step, step), :], ring.at[slot, b, pl.ds(q * step, step), :], ring_sem.at[slot, b * 4 + q]))
-        return out
-
-    def shared_copies(slot, i):
-        return pair_copies(slot, sg.at[:, pl.ds(i * ff, ff)], su.at[:, pl.ds(i * ff, ff)])
-
-    def expert_copies(slot, e):
-        return pair_copies(slot, eg.at[e], eu.at[e])
-
-    def tile_at(slot, i):
-        return ring.at[slot, i // 5, pl.ds(0, ff), pl.ds((i % 5) * CHUNK, CHUNK)]
-
-    def down_copies(slot, j):
-        cols = pl.ds(pl.multiple_of(j * CHUNK, CHUNK), CHUNK)
-        out = [pltpu.make_async_copy(ed.at[e, :, cols], tile_at(slot, e), ring_sem.at[slot, e]) for e in range(n_exp)]
-        for i in range(2):
-            out.append(pltpu.make_async_copy(sd.at[pl.ds(i * ff, ff), cols], tile_at(slot, n_exp + i), ring_sem.at[slot, n_exp + i]))
-        return out
-
     def start(copies):
         for c in copies:
             c.start()
@@ -275,35 +255,117 @@
         for c in copies:
             c.wait()
 
+    step = deep // 2
+
+    def block_copies(slot, gate, up, k, col):
+        out = []
+        for b, src in enumerate((gate, up)):
+            for q in range(2):
+                at = pl.ds(pl.multiple_of(k * deep + q * step, step), step)
+                out.append(pltpu.make_async_copy(src.at[at, col], ring.at[slot, b, pl.ds(q * step, step), :], ring_sem.at[slot, 2 * b + q]))
+        return out
+
+    def half_copies(i):
+        e = i % n_exp
+        return block_copies(i % 4, eg.at[e], eu.at[e], i // n_exp, slice(None))
+
+    def shared_copies(q, i):
+        col = pl.ds(pl.multiple_of(i * ff, side), ff)
+        return block_copies(2 * q, sg, su, 0, col) + block_copies(2 * q + 1, sg, su, 1, col)
+
+    def tile(q, g, lo, size):
+        return ring.at[2 * q + g // 10, (g // 5) % 2, pl.ds(lo, size), pl.ds((g % 5) * CHUNK, CHUNK)]
+
+    def pair_sem(q, i):
+        return ring_sem.at[2 * q + i // 8, i % 8]
+
+    def down_tiles(q, e):
+        return tile(q, e, 0, deep), tile(q, n_exp + e // 2, (e % 2) * left, left)
+
+    def down_copies(j):
+        q = j % 2
+        cols = pl.ds(pl.multiple_of(j * CHUNK, CHUNK), CHUNK)
+        out = []
+        for e in range(n_exp):
+            head, tail = down_tiles(q, e)
+            out.append(pltpu.make_async_copy(ed.at[e, pl.ds(0, deep), cols], head, pair_sem(q, 2 * e)))
+            out.append(pltpu.make_async_copy(ed.at[e, pl.ds(deep, left), cols], tail, pair_sem(q, 2 * e + 1)))
+        return out
+
+    def shared_tiles(q, c, i):
+        return tile(q, 3 * c + i, 0, deep), tile(q, 3 * c + 2, i * left, left)
+
+    def shared_down_copies(t):
+        out = []
+        for c in range(4):
+            cols = pl.ds(pl.multiple_of((4 * t + c) * CHUNK, CHUNK), CHUNK)
+            for i in range(2):
+                head, tail = shared_tiles(t, c, i)
+                out.append(pltpu.make_async_copy(sd.at[pl.ds(i * ff, deep), cols], head, pair_sem(t, 4 * c + 2 * i)))
+                out.append(pltpu.make_async_copy(sd.at[pl.ds(i * ff + deep, left), cols], tail, pair_sem(t, 4 * c + 2 * i + 1)))
+        return out
+
     barrier = pltpu.get_barrier_semaphore()
     for _, _, dev in others:
         pl.semaphore_signal(barrier, inc=1, device_id={'ep': dev}, device_id_type=pl.DeviceIdType.MESH)
+    in_copies = [pltpu.make_async_copy(h_hbm.at[k], hall.at[0, k, pl.ds(0, rows)], in_sem.at[k]) for k in range(2)]
+    in_copies.append(pltpu.make_async_copy(rw_hbm, rw_ref, in_sem.at[2]))
+    res_copy = pltpu.make_async_copy(res_hbm, out_ref, in_sem.at[3])
+    start(in_copies)
+    wait(in_copies)
     start(shared_copies(0, 0))
     start(shared_copies(1, 1))
-    start(expert_copies(2, 0))
-    res_copy = pltpu.make_async_copy(res_hbm, out_ref, res_sem)
     res_copy.start()
     pl.semaphore_wait(barrier, len(others))
 
     part_a, part_b = pl.ds(0, half), pl.ds(half, half)
     own, other = pl.ds(0, rows), pl.ds(rows, rows)
     rw_copies = [remote(rw_ref.at[pl.ds(pl.multiple_of(dev * n_exp, n_exp), n_exp), :], rwin.at[r, p], rw_s.at[i], rw_r.at[i], dev) for i, (r, p, dev) in enumerate(others)]
+
+    class Gather:
+        def __init__(self, k):
+            def hop(i, src, dst, dev):
+                return remote(src, dst, ag_s.at[k, i], ag_r.at[k, i], dev)
+            self.mate = hop(0, hall.at[0, k, own], hall.at[0, k, other], mate)
+            self.x_a = hop(1, hall.at[0, k, part_a], hall.at[1, k, part_a], xn)
+            self.x_b = hop(2, hall.at[0, k, part_b], hall.at[1, k, part_b], xn)
+            self.y_b = hop(3, hall.at[0, k, part_b], hall.at[2, k, part_b], yn)
+            self.y_a = hop(4, hall.at[0, k, part_a], hall.at[2, k, part_a], yn)
+            self.d_a = hop(5, hall.at[1, k, part_a], hall.at[3, k, part_a], yn)
+            self.d_b = hop(6, hall.at[2, k, part_b], hall.at[3, k, part_b], xn)
+            self.m_x = hop(7, hall.at[1, k, own], hall.at[1, k, other], mate)
+            self.m_y = hop(8, hall.at[2, k, own], hall.at[2, k, other], mate)
+            self.m_da = hop(9, hall.at[3, k, part_a], hall.at[3, k, pl.ds(rows, half)], mate)
+            self.m_db = hop(10, hall.at[3, k, part_b], hall.at[3, k, pl.ds(rows + half, half)], mate)
+
+        def send(self):
+            start([self.x_a, self.y_b, self.x_b, self.y_a, self.mate])
+
+        def turn(self):
+            self.x_a.wait_recv()
+            self.d_a.start()
+            self.y_b.wait_recv()
+            self.d_b.start()
+
+        def share(self):
+            self.x_b.wait_recv()
+            self.m_x.start()
+            self.y_a.wait_recv()
+            self.m_y.start()
+
+        def last(self):
+            self.d_a.wait_recv()
+            self.m_da.start()
+            self.d_b.wait_recv()
+            self.m_db.start()
+
+        def sends(self):
+            return [self.mate, self.x_a, self.x_b, self.y_b, self.y_a, self.d_a, self.d_b, self.m_x, self.m_y, self.m_da, self.m_db]
+
+    ga, gb = Gather(0), Gather(1)
+    ga.send()
     start(rw_copies)
-    to_mate = remote(h_ref, hall.at[0, other], ag_s.at[0], ag_r.at[0], mate)
-    x_a = remote(h_ref.at[part_a], hall.at[1, part_a], ag_s.at[1], ag_r.at[1], xn)
-    x_b = remote(h_ref.at[part_b], hall.at[1, part_b], ag_s.at[2], ag_r.at[2], xn)
-    y_b = remote(h_ref.at[part_b], hall.at[2, part_b], ag_s.at[3], ag_r.at[3], yn)
-    y_a = remote(h_ref.at[part_a], hall.at[2, part_a], ag_s.at[4], ag_r.at[4], yn)
-    d_a = remote(hall.at[1, part_a], hall.at[3, part_a], ag_s.at[5], ag_r.at[5], yn)
-    d_b = remote(hall.at[2, part_b], hall.at[3, part_b], ag_s.at[6], ag_r.at[6], xn)
-    m_x = remote(hall.at[1, own], hall.at[1, other], ag_s.at[7], ag_r.at[7], mate)
-    m_y = remote(hall.at[2, own], hall.at[2, other], ag_s.at[8], ag_r.at[8], mate)
-    m_da = remote(hall.at[3, part_a], hall.at[3, pl.ds(rows, half)], ag_s.at[9], ag_r.at[9], mate)
-    m_db = remote(hall.at[3, part_b], hall.at[3, pl.ds(rows + half, half)], ag_s.at[10], ag_r.at[10], mate)
-    for c in (x_a, y_b, to_mate, x_b, y_a):
-        c.start()
-
-    hall[0, 0:rows, :] = h_ref[...]
+
     rwin[0, 0] = rw_ref[pl.ds(pl.multiple_of(me * n_exp, n_exp), n_exp), :]
     for c in rw_copies:
         c.wait_recv()
@@ -331,154 +393,187 @@
         pw[r, 1] = mid
         pw[r, 2] = (rest - mid.astype(F32)).astype(BF16)
 
-    def gather_rows(r):
+    def gather_rows(r, k):
         wide = 512
-        for n in range(0, d_model, wide):
-            got = jnp.dot(pbuf[r], hall[r, :, n:n + wide], preferred_element_type=F32).astype(BF16)
+        for n in range(0, deep, wide):
+            got = jnp.dot(pbuf[r], hall[r, k, :, n:n + wide], preferred_element_type=F32).astype(BF16)
             for e in range(n_exp):
-                xbuf[e, r * grp:(r + 1) * grp, n:n + wide] = got[e * grp:(e + 1) * grp, :]
-
-    def shared_item(i):
+                xbuf[k, e, r * grp:(r + 1) * grp, n:n + wide] = got[e * grp:(e + 1) * grp, :]
+
+    def shared_hidden(i):
         wait(shared_copies(i, i))
         for n, w in mids:
-            g = jnp.dot(h_ref[...], ring[i, 0, :, n:n + w], preferred_element_type=F32)
-            u = jnp.dot(h_ref[...], ring[i, 1, :, n:n + w], preferred_element_type=F32)
-            actsh[i, :, n:n + w] = (jax.nn.silu(g) * u).astype(BF16)
-        start(expert_copies(i, i + 1))
+            vals = []
+            for b in range(2):
+                v = jnp.dot(hall[0, 0, 0:rows, :], ring[2 * i, b, :, n:n + w], preferred_element_type=F32)
+                vals.append(v + jnp.dot(hall[0, 1, 0:rows, :], ring[2 * i + 1, b, :, n:n + w], preferred_element_type=F32))
+            actsh[i, :, n:n + w] = (jax.nn.silu(vals[0]) * vals[1]).astype(BF16)
+        for k in range(2):
+            start(half_copies(2 * i + k))
 
     for r in range(4):
         tables(r)
-    to_mate.wait_recv()
-    gather_rows(0)
-    shared_item(0)
-    x_a.wait_recv()
-    d_a.start()
-    y_b.wait_recv()
-    d_b.start()
-    shared_item(1)
-    x_b.wait_recv()
-    m_x.start()
-    y_a.wait_recv()
-    m_y.start()
-    m_x.wait_recv()
-    gather_rows(1)
-    m_y.wait_recv()
-    gather_rows(2)
-    d_a.wait_recv()
-    m_da.start()
-    d_b.wait_recv()
-    m_db.start()
-    m_da.wait_recv()
-    m_db.wait_recv()
-    gather_rows(3)
-    res_copy.wait()
+    ga.turn()
+    gb.send()
+    shared_hidden(0)
+    ga.share()
+    ga.mate.wait_recv()
+    gather_rows(0, 0)
+    shared_hidden(1)
+    ga.last()
+    ga.m_x.wait_recv()
+    gather_rows(1, 0)
+    ga.m_y.wait_recv()
+    gather_rows(2, 0)
+    ga.m_da.wait_recv()
+    ga.m_db.wait_recv()
+    gather_rows(3, 0)
 
     @pl.loop(0, n_exp)
     def _(e):
-        slot = (e + 2) % 3
-        wait(expert_copies(slot, e))
+        slot = e % 4
+        wait(half_copies(e))
         for n, w in mids:
-            g = jnp.dot(xbuf[e], ring[slot, 0, :, n:n + w], preferred_element_type=F32)
-            u = jnp.dot(xbuf[e], ring[slot, 1, :, n:n + w], preferred_element_type=F32)
-            actt[:, n:n + w] = (jax.nn.silu(g) * u).astype(BF16)
-        xbuf[e, :, 0:ff] = actt[...]
-
-        @pl.when(e + 3 < n_exp)
+            part[e, :, n:n + w] = jnp.dot(xbuf[0, e], ring[slot, 0, :, n:n + w], preferred_element_type=F32)
+            part[e, :, ff + n:ff + n + w] = jnp.dot(xbuf[0, e], ring[slot, 1, :, n:n + w], preferred_element_type=F32)
+        start(half_copies(e + 4))
+
+        @pl.when(e == 0)
         def _():
-            start(expert_copies(slot, e + 3))
-
-        @pl.when(e + 3 >= n_exp)
+            gb.turn()
+            gb.mate.wait_recv()
+            gather_rows(0, 1)
+
+        @pl.when(e == 2)
         def _():
-            start(down_copies(slot, e + 3 - n_exp))
-
-    side = CHUNK // 2
+            gb.share()
+
+        @pl.when(e == 3)
+        def _():
+            gb.m_x.wait_recv()
+            gather_rows(1, 1)
+            gb.m_y.wait_recv()
+            gather_rows(2, 1)
+
+        pl.when(e == 4)(gb.last)
+
+        @pl.when(e == 5)
+        def _():
+            gb.m_da.wait_recv()
+            gb.m_db.wait_recv()
+            gather_rows(3, 1)
+
+    @pl.loop(0, n_exp)
+    def _(e):
+        slot = e % 4
+        wait(half_copies(n_exp + e))
+        late = []
+        for n, w in mids:
+            g = part[e, :, n:n + w] + jnp.dot(xbuf[1, e], ring[slot, 0, :, n:n + w], preferred_element_type=F32)
+            u = part[e, :, ff + n:ff + n + w] + jnp.dot(xbuf[1, e], ring[slot, 1, :, n:n + w], preferred_element_type=F32)
+            act = (jax.nn.silu(g) * u).astype(BF16)
+            if n < deep:
+                xbuf[0, e, :, n:n + w] = act
+            else:
+                late.append((n - deep, w, act))
+        for n, w, act in late:
+            xbuf[1, e, :, n:n + w] = act
+        pl.when(e < 4)(lambda: start(half_copies(n_exp + e + 4)))
+        pl.when(e == 5)(lambda: start(down_copies(0)))
+        pl.when(e == 7)(lambda: start(down_copies(1)))
+
+    def acc(j, f, r):
+        return part.at[j, pl.ds(0, rows), pl.ds((4 * f + r) * side, side)]
+
+    def base(j, f):
+        return part.at[j, pl.ds(0, rows), pl.ds((8 + f) * side, side)]
 
     def first_stage(j):
         out = []
         for f, dev in enumerate((xn, yn)):
             for q, r in enumerate((1 + f, 3)):
-                out.append(remote(acc.at[j, f, r], r1.at[j, f, q], s1_s.at[j, 2 * f + q], s1_r.at[j, 2 * f + q], dev))
+                out.append(remote(acc(j, f, r), r1.at[j, f, q], s1_s.at[j, 2 * f + q], s1_r.at[j, 2 * f + q], dev))
         return out
 
     def second_stage(j):
-        return [remote(acc.at[j, f, 2 - f], r2.at[j, f], s2_s.at[j, f], s2_r.at[j, f], dev) for f, dev in enumerate((yn, xn))]
+        return [remote(acc(j, f, 2 - f), r2.at[j, f], s2_s.at[j, f], s2_r.at[j, f], dev) for f, dev in enumerate((yn, xn))]
 
     def swap(j):
         return remote(stage.at[j % 2], drecv.at[j], d_s.at[j], d_r.at[j], mate)
 
     def send_sum(j):
         swap(j).wait_recv()
-        acc[j] = acc[j] + drecv[j]
+        for f in range(2):
+            for r in range(4):
+                acc(j, f, r)[...] = acc(j, f, r)[...] + drecv[j, f, r]
         start(first_stage(j))
 
     def pass_on(j):
         for c in first_stage(j):
             c.wait_recv()
         for f, c in enumerate(second_stage(j)):
-            acc[j, f, 2 - f] = acc[j, f, 2 - f] + r1[j, f, 1]
+            acc(j, f, 2 - f)[...] = acc(j, f, 2 - f)[...] + r1[j, f, 1]
             c.start()
         for f in range(2):
-            cut = slice(f * side, (f + 1) * side)
-            base[j, :, cut] = base[j, :, cut] + (acc[j, f, 0] + r1[j, f, 0])
+            acc(j, f, 0)[...] = acc(j, f, 0)[...] + r1[j, f, 0]
 
     @pl.loop(0, n_chunk)
     def _(j):
-        slot = (j + n_exp + 2) % 3
-        wait(down_copies(slot, j))
+        q = j % 2
+        wait(down_copies(j))
         for e in range(n_exp):
-            if e == n_exp // 2:
-                pl.when(j >= 2)(lambda: send_sum(j - 1))
-            tile = ring[slot, e // 5, 0:ff, (e % 5) * CHUNK:(e % 5 + 1) * CHUNK]
-            got = jnp.dot(xbuf[e, :, 0:ff], tile, preferred_element_type=F32).astype(BF16)
+            if e == 3:
+                pl.when(j >= 1)(lambda: send_sum(j - 1))
+            head, tail = down_tiles(q, e)
+            got = jnp.dot(xbuf[0, e], head[...], preferred_element_type=F32)
+            got = (got + jnp.dot(xbuf[1, e, :, 0:left], tail[...], preferred_element_type=F32)).astype(BF16)
             for r in range(4):
-                ebuf[r, e * grp:(e + 1) * grp, :] = got[r * grp:(r + 1) * grp, :]
-
-        @pl.when(j >= 2)
-        def _():
-            swap(j - 2).wait_send()
-
+                pbuf[r, e * grp:(e + 1) * grp, :] = got[r * grp:(r + 1) * grp, :]
+        pl.when(j >= 2)(lambda: swap(j - 2).wait_send())
         for r in range(4):
-            part = jnp.dot(pw[r, 0], ebuf[r], preferred_element_type=F32)
-            part = part + jnp.dot(pw[r, 1], ebuf[r], preferred_element_type=F32)
-            part = part + jnp.dot(pw[r, 2], ebuf[r], preferred_element_type=F32)
+            out = jnp.dot(pw[r, 0], pbuf[r], preferred_element_type=F32)
+            out = out + jnp.dot(pw[r, 1], pbuf[r], preferred_element_type=F32)
+            out = out + jnp.dot(pw[r, 2], pbuf[r], preferred_element_type=F32)
             for f in range(2):
                 cut = slice(f * side, (f + 1) * side)
-                acc[j, f, r] = part[0:rows, cut]
-                stage[j % 2, f, r] = part[rows:, cut]
+                acc(j, f, r)[...] = out[0:rows, cut]
+                stage[q, f, r] = out[rows:, cut]
         swap(j).start()
-
-        cols = pl.ds(pl.multiple_of(j * CHUNK, CHUNK), CHUNK)
-        total = out_ref[:, cols].astype(F32)
-        for i in range(2):
-            k = n_exp + i
-            tile = ring[slot, k // 5, 0:ff, (k % 5) * CHUNK:(k % 5 + 1) * CHUNK]
-            total = total + jnp.dot(actsh[i], tile, preferred_element_type=F32)
-        base[j] = total
-
-        @pl.when(j + 3 < n_chunk)
-        def _():
-            start(down_copies(slot, j + 3))
-
-        pl.when(j == 0)(lambda: send_sum(0))
-
-        @pl.when(j >= LAG)
-        def _():
-            pass_on(j - LAG)
+        pl.when(j + 2 < n_chunk)(lambda: start(down_copies(j + 2)))
+        pl.when(j == n_chunk - 2)(lambda: start(shared_down_copies(0)))
+        pl.when(j == n_chunk - 1)(lambda: start(shared_down_copies(1)))
+        pl.when(j >= LAG)(lambda: pass_on(j - LAG))
 
     send_sum(n_chunk - 1)
-
-    @pl.loop(n_chunk - LAG, n_chunk)
-    def _(j):
-        pass_on(j)
+    pass_on(n_chunk - 4)
+    pass_on(n_chunk - 3)
+
+
+    res_copy.wait()
+
+    @pl.loop(0, 2)
+    def _(t):
+        wait(shared_down_copies(t))
+        for c in range(4):
+            j = 4 * t + c
+            cols = pl.ds(pl.multiple_of(j * CHUNK, CHUNK), CHUNK)
+            total = out_ref[:, cols].astype(F32)
+            for i in range(2):
+                head, tail = shared_tiles(t, c, i)
+                total = total + jnp.dot(actsh[i, :, 0:deep], head[...], preferred_element_type=F32)
+                total = total + jnp.dot(actsh[i, :, deep:ff], tail[...], preferred_element_type=F32)
+            for f in range(2):
+                base(j, f)[...] = total[:, f * side:(f + 1) * side]
+        pass_on(n_chunk - 2 + t)
 
     @pl.loop(0, n_chunk)
     def _(j):
         for f, c in enumerate(second_stage(j)):
             c.wait_recv()
-            cut = slice(f * side, (f + 1) * side)
-            out_ref[:, pl.ds(pl.multiple_of(j * CHUNK + f * side, side), side)] = (base[j, :, cut] + r2[j, f]).astype(BF16)
-
-    for c in rw_copies + [to_mate, x_a, x_b, y_a, y_b, d_a, d_b, m_x, m_y, m_da, m_db]:
+            cols = pl.ds(pl.multiple_of(j * CHUNK + f * side, side), side)
+            out_ref[:, cols] = (base(j, f)[...] + (acc(j, f, 0)[...] + r2[j, f])).astype(BF16)
+
+    for c in rw_copies + ga.sends() + gb.sends():
         c.wait_send()
     swap(n_chunk - 2).wait_send()
     swap(n_chunk - 1).wait_send()
@@ -490,37 +585,38 @@
 
 
 def moe(h, table, resid, eg, eu, ed, sg, su, sd):
-    rows, d_model = h.shape
+    _, rows, deep = h.shape
+    d_model = 2 * deep
     n_exp, _, ff = eg.shape
     n_chunk = d_model // CHUNK
+    side = CHUNK // 2
     slots = 8 * CAP
+    pairs = 2 * CAP * n_exp
     vmem = pl.BlockSpec(memory_space=pltpu.VMEM)
     hbm = pl.BlockSpec(memory_space=pl.ANY)
     dma = pltpu.SemaphoreType.DMA
     scratch = [
-        pltpu.VMEM((3, 2, d_model, ff), BF16),
-        pltpu.VMEM((4, 2 * rows, d_model), BF16),
-        pltpu.VMEM((n_exp, slots, d_model), BF16),
-        pltpu.VMEM((slots, ff), BF16),
+        pltpu.VMEM((4, 2, deep, ff), BF16),
+        pltpu.VMEM((4, 2, 2 * rows, deep), BF16),
+        pltpu.VMEM((2, n_exp, slots, deep), BF16),
+        pltpu.VMEM((n_exp, slots, 2 * ff), F32),
         pltpu.VMEM((2, rows, ff), BF16),
-        pltpu.VMEM((n_chunk, 2, 4, rows, CHUNK // 2), F32),
-        pltpu.VMEM((n_chunk, 2, 4, rows, CHUNK // 2), F32),
-        pltpu.VMEM((n_chunk, 2, 2, rows, CHUNK // 2), F32),
-        pltpu.VMEM((n_chunk, 2, rows, CHUNK // 2), F32),
-        pltpu.VMEM((2, 2, 4, rows, CHUNK // 2), F32),
-        pltpu.VMEM((n_chunk, rows, CHUNK), F32),
-        pltpu.VMEM((4, 3, 2 * rows, n_exp * 2 * CAP), BF16),
-        pltpu.VMEM((n_exp * 2 * CAP, 2 * rows), F32),
-        pltpu.VMEM((4, n_exp * 2 * CAP, 2 * rows), BF16),
-        pltpu.VMEM((4, n_exp * 2 * CAP, CHUNK), BF16),
+        pltpu.VMEM((n_chunk, 2, 4, rows, side), F32),
+        pltpu.VMEM((n_chunk, 2, 2, rows, side), F32),
+        pltpu.VMEM((n_chunk, 2, rows, side), F32),
+        pltpu.VMEM((2, 2, 4, rows, side), F32),
+        pltpu.VMEM((4, 3, 2 * rows, pairs), BF16),
+        pltpu.VMEM((pairs, 2 * rows), F32),
+        pltpu.VMEM((4, pairs, 2 * rows), BF16),
         pltpu.VMEM((4, 2, n_exp, rows), F32),
-        dma((3, 10)), dma, dma((11,)), dma((11,)), dma((7,)), dma((7,)), dma((n_chunk,)), dma((n_chunk,)),
+        pltpu.VMEM(table.shape, F32),
+        dma((4, 8)), dma((4,)), dma((2, 11)), dma((2, 11)), dma((7,)), dma((7,)), dma((n_chunk,)), dma((n_chunk,)),
         dma((n_chunk, 4)), dma((n_chunk, 4)), dma((n_chunk, 2)), dma((n_chunk, 2)),
     ]
     return pl.pallas_call(
         moe_kernel,
         out_shape=jax.ShapeDtypeStruct((rows, d_model), BF16),
-        in_specs=[vmem] * 2 + [hbm] * 7,
+        in_specs=[hbm] * 9,
         out_specs=vmem,
         scratch_shapes=scratch,
         compiler_params=pltpu.CompilerParams(collective_id=0, has_side_effects=True, vmem_limit_bytes=67043328),

time: 124 us -> 120 us (0.968)
  Pallas kernels: 122 us -> 117 us
    pallas_call x1, Pallas kernels: 95.8 us -> 91.1 us  [moe(): pl.pallas_call(moe_kernel, out_shape=jax.ShapeDtypeStruct((rows, d_model)...]
where the time goes in v4:
time: 120 us; the launch traced here: 119 us
  Pallas kernels  117 us (98%)
  local copies, waits for them, and re-layouts  1.88 us (2%)
    pallas_call x1, Pallas kernels, moe(): pl.pallas_call(moe_kernel, out_shape=jax.ShapeDtypeStruct((rows, d_model)...  91.1 us
    pallas_call x1, Pallas kernels, attention(): pl.pallas_call(attn_kernel, out_shape=(jax.ShapeDtypeStruct(lat_cache.sha...  25.7 us

profile of v4, /device:TPU:0, one launch (start us, length us, event | category | flops | bytes accessed | tf_op | source)
XLA Modules:
  0.0 119.3 jit_solution(6058296332296537758)
XLA Ops:
  0.6 25.7 %shard_map.202 = (bf16[128,128,512]{2,1,0:T(8,128)(2,1)}, bf16[128,64,128]{2,1,0:T(8,128)(2,1)}, bf16[128,2048]{1,0:T(8,128)(2,1)}, bf16[2,128,1024]{2,1,0:T(8,128)(2,1)}, f32[64,128]{1,0:T(8,128)}) custom-call(s32[128]{0:T(128)} %pos_ref.1, s32[1,128]{1,0:T(1,128)} %bitcast.10, bf16[128,2048]{1,0:T(8,128)(2,1)} %x_ref.1, bf16[2048]{0:T(1024)(128)(2,1)} %gain_ref.1, ...), custom_call_target="tpu_custom_call" | custom-call | flops 5000000000 | bytes 66000000 | tf_op jit(solution)/shard_map/pallas_call | solution.py:204
  26.3 91.1 %shard_map.203 = bf16[128,2048]{1,0:T(8,128)(2,1)} custom-call(bf16[2,128,1024]{2,1,0:T(8,128)(2,1)} %get-tuple-element.8.h_hbm, f32[64,128]{1,0:T(8,128)} %get-tuple-element.9.rw_hbm, bf16[128,2048]{1,0:T(8,128)(2,1)} %get-tuple-element.10.res_hbm, bf16[8,2048,1408]{2,1,0:T(8,128)(2,1)} %eg.1, bf16[8,2048,1408]{2,1,0:T(8,128)(2,1)} %eu.1, ...), custom_call_target="tpu_custom_call" | custom-call | flops 40000000000 | bytes 175000000 | tf_op jit(solution)/shard_map/pallas_call | solution.py:616
  117.5 1.9 %copy.23 = bf16[128,2048]{1,0:T(8,128)(2,1)} copy(bf16[128,2048]{1,0:T(8,128)(2,1)} %shard_map.203) | data formatting | bytes 1048576

commit v5 on v4

--- a/solution.py
+++ b/solution.py
@@ -12,7 +12,7 @@
 CAP = 24
 CHUNK = 256
 BLK = 16
-LAG = 4
+LAG = 2
 F32 = jnp.float32
 BF16 = jnp.bfloat16
 
@@ -522,13 +522,12 @@
         q = j % 2
         wait(down_copies(j))
         for e in range(n_exp):
-            if e == 3:
-                pl.when(j >= 1)(lambda: send_sum(j - 1))
             head, tail = down_tiles(q, e)
             got = jnp.dot(xbuf[0, e], head[...], preferred_element_type=F32)
             got = (got + jnp.dot(xbuf[1, e, :, 0:left], tail[...], preferred_element_type=F32)).astype(BF16)
             for r in range(4):
                 pbuf[r, e * grp:(e + 1) * grp, :] = got[r * grp:(r + 1) * grp, :]
+        pl.when(j >= 1)(lambda: send_sum(j - 1))
         pl.when(j >= 2)(lambda: swap(j - 2).wait_send())
         for r in range(4):
             out = jnp.dot(pw[r, 0], pbuf[r], preferred_element_type=F32)
@@ -545,8 +544,6 @@
         pl.when(j >= LAG)(lambda: pass_on(j - LAG))
 
     send_sum(n_chunk - 1)
-    pass_on(n_chunk - 4)
-    pass_on(n_chunk - 3)
 
 
     res_copy.wait()

time: 120 us -> 116 us (0.967)
  Pallas kernels: 117 us -> 114 us
    pallas_call x1, Pallas kernels: 91.1 us -> 88 us  [moe(): pl.pallas_call(moe_kernel, out_shape=jax.ShapeDtypeStruct((rows, d_model)...]
where the time goes in v5:
time: 116 us
  Pallas kernels  114 us (98%)
  local copies, waits for them, and re-layouts  1.88 us (2%)
    pallas_call x1, Pallas kernels, moe(): pl.pallas_call(moe_kernel, out_shape=jax.ShapeDtypeStruct((rows, d_model)...  88 us
    pallas_call x1, Pallas kernels, attention(): pl.pallas_call(attn_kernel, out_shape=(jax.ShapeDtypeStruct(lat_cache.sha...  25.7 us

profile of v5, /device:TPU:0, one launch (start us, length us, event | category | flops | bytes accessed | tf_op | source)
XLA Modules:
  0.0 116.2 jit_solution(9196647557088336696)
XLA Ops:
  0.6 25.7 %shard_map.202 = (bf16[128,128,512]{2,1,0:T(8,128)(2,1)}, bf16[128,64,128]{2,1,0:T(8,128)(2,1)}, bf16[128,2048]{1,0:T(8,128)(2,1)}, bf16[2,128,1024]{2,1,0:T(8,128)(2,1)}, f32[64,128]{1,0:T(8,128)}) custom-call(s32[128]{0:T(128)} %pos_ref.1, s32[1,128]{1,0:T(1,128)} %bitcast.10, bf16[128,2048]{1,0:T(8,128)(2,1)} %x_ref.1, bf16[2048]{0:T(1024)(128)(2,1)} %gain_ref.1, ...), custom_call_target="tpu_custom_call" | custom-call | flops 5000000000 | bytes 66000000 | tf_op jit(solution)/shard_map/pallas_call | solution.py:204
  26.3 88.0 %shard_map.203 = bf16[128,2048]{1,0:T(8,128)(2,1)} custom-call(bf16[2,128,1024]{2,1,0:T(8,128)(2,1)} %get-tuple-element.8.h_hbm, f32[64,128]{1,0:T(8,128)} %get-tuple-element.9.rw_hbm, bf16[128,2048]{1,0:T(8,128)(2,1)} %get-tuple-element.10.res_hbm, bf16[8,2048,1408]{2,1,0:T(8,128)(2,1)} %eg.1, bf16[8,2048,1408]{2,1,0:T(8,128)(2,1)} %eu.1, ...), custom_call_target="tpu_custom_call" | custom-call | flops 40000000000 | bytes 175000000 | tf_op jit(solution)/shard_map/pallas_call | solution.py:613
  114.3 1.9 %copy.23 = bf16[128,2048]{1,0:T(8,128)(2,1)} copy(bf16[128,2048]{1,0:T(8,128)(2,1)} %shard_map.203) | data formatting | bytes 1048576

commit v6 on v5

--- a/solution.py
+++ b/solution.py
@@ -220,9 +220,9 @@
     return resid, h, table, lat_out, jnp.swapaxes(rope_out, 1, 2)
 
 
-def moe_kernel(h_hbm, rw_hbm, res_hbm, eg, eu, ed, sg, su, sd, out_ref,
-               ring, hall, xbuf, part, actsh, drecv, r1, r2, stage, pw, pwf, pbuf, rwin, rw_ref,
-               ring_sem, in_sem, ag_s, ag_r, rw_s, rw_r, d_s, d_r, s1_s, s1_r, s2_s, s2_r):
+def moe_kernel(h_hbm, rw_hbm, res_hbm, eg, eu, ed, sg, su, sd, out_hbm,
+               ring, hall, xbuf, part, actsh, drecv, r1, r2, stage, pw, pwf, pbuf, rwin, rw_ref, out_ref,
+               ring_sem, in_sem, out_sem, ag_s, ag_r, rw_s, rw_r, d_s, d_r, s1_s, s1_r, s2_s, s2_r):
     rows = rw_hbm.shape[1]
     half = rows // 2
     deep = h_hbm.shape[2]
@@ -563,12 +563,17 @@
                 base(j, f)[...] = total[:, f * side:(f + 1) * side]
         pass_on(n_chunk - 2 + t)
 
+    def out_copy(j):
+        cols = pl.ds(pl.multiple_of(j * CHUNK, CHUNK), CHUNK)
+        return pltpu.make_async_copy(out_ref.at[:, cols], out_hbm.at[:, cols], out_sem.at[j])
+
     @pl.loop(0, n_chunk)
     def _(j):
         for f, c in enumerate(second_stage(j)):
             c.wait_recv()
             cols = pl.ds(pl.multiple_of(j * CHUNK + f * side, side), side)
             out_ref[:, cols] = (base(j, f)[...] + (acc(j, f, 0)[...] + r2[j, f])).astype(BF16)
+        out_copy(j).start()
 
     for c in rw_copies + ga.sends() + gb.sends():
         c.wait_send()
@@ -579,6 +584,7 @@
     def _(j):
         for c in first_stage(j) + second_stage(j):
             c.wait_send()
+        out_copy(j).wait()
 
 
 def moe(h, table, resid, eg, eu, ed, sg, su, sd):
@@ -589,7 +595,6 @@
     side = CHUNK // 2
     slots = 8 * CAP
     pairs = 2 * CAP * n_exp
-    vmem = pl.BlockSpec(memory_space=pltpu.VMEM)
     hbm = pl.BlockSpec(memory_space=pl.ANY)
     dma = pltpu.SemaphoreType.DMA
     scratch = [
@@ -607,14 +612,15 @@
         pltpu.VMEM((4, pairs, 2 * rows), BF16),
         pltpu.VMEM((4, 2, n_exp, rows), F32),
         pltpu.VMEM(table.shape, F32),
-        dma((4, 8)), dma((4,)), dma((2, 11)), dma((2, 11)), dma((7,)), dma((7,)), dma((n_chunk,)), dma((n_chunk,)),
+        pltpu.VMEM((rows, d_model), BF16),
+        dma((4, 8)), dma((4,)), dma((n_chunk,)), dma((2, 11)), dma((2, 11)), dma((7,)), dma((7,)), dma((n_chunk,)), dma((n_chunk,)),
         dma((n_chunk, 4)), dma((n_chunk, 4)), dma((n_chunk, 2)), dma((n_chunk, 2)),
     ]
     return pl.pallas_call(
         moe_kernel,
         out_shape=jax.ShapeDtypeStruct((rows, d_model), BF16),
         in_specs=[hbm] * 9,
-        out_specs=vmem,
+        out_specs=hbm,
         scratch_shapes=scratch,
         compiler_params=pltpu.CompilerParams(collective_id=0, has_side_effects=True, vmem_limit_bytes=67043328),
         cost_estimate=pl.CostEstimate(flops=40_000_000_000, bytes_accessed=175_000_000, transcendentals=0),

time: 116 us -> 116 us (level)
  no operation moved by 1% of the time
where the time goes in v6:
time: 116 us
  Pallas kernels  113 us (97%)
  local copies, waits for them, and re-layouts  1.88 us (2%)
    pallas_call x1, Pallas kernels, moe(): pl.pallas_call(moe_kernel, out_shape=jax.ShapeDtypeStruct((rows, d_model)...  87.7 us
    pallas_call x1, Pallas kernels, attention(): pl.pallas_call(attn_kernel, out_shape=(jax.ShapeDtypeStruct(lat_cache.sha...  25.7 us

profile of v6, /device:TPU:0, one launch (start us, length us, event | category | flops | bytes accessed | tf_op | source)
XLA Modules:
  0.0 115.9 jit_solution(11189425595803414097)
XLA Ops:
  0.6 25.7 %shard_map.202 = (bf16[128,128,512]{2,1,0:T(8,128)(2,1)}, bf16[128,64,128]{2,1,0:T(8,128)(2,1)}, bf16[128,2048]{1,0:T(8,128)(2,1)}, bf16[2,128,1024]{2,1,0:T(8,128)(2,1)}, f32[64,128]{1,0:T(8,128)}) custom-call(s32[128]{0:T(128)} %pos_ref.1, s32[1,128]{1,0:T(1,128)} %bitcast.10, bf16[128,2048]{1,0:T(8,128)(2,1)} %x_ref.1, bf16[2048]{0:T(1024)(128)(2,1)} %gain_ref.1, ...), custom_call_target="tpu_custom_call" | custom-call | flops 5000000000 | bytes 66000000 | tf_op jit(solution)/shard_map/pallas_call | solution.py:204
  26.3 87.7 %shard_map.203 = bf16[128,2048]{1,0:T(8,128)(2,1)} custom-call(bf16[2,128,1024]{2,1,0:T(8,128)(2,1)} %get-tuple-element.8.h_hbm, f32[64,128]{1,0:T(8,128)} %get-tuple-element.9.rw_hbm, bf16[128,2048]{1,0:T(8,128)(2,1)} %get-tuple-element.10.res_hbm, bf16[8,2048,1408]{2,1,0:T(8,128)(2,1)} %eg.1, bf16[8,2048,1408]{2,1,0:T(8,128)(2,1)} %eu.1, ...), custom_call_target="tpu_custom_call" | custom-call | flops 40000000000 | bytes 175000000 | tf_op jit(solution)/shard_map/pallas_call | solution.py:619
  114.0 1.9 %copy.23 = bf16[128,2048]{1,0:T(8,128)(2,1)} copy(bf16[128,2048]{1,0:T(8,128)(2,1)} %shard_map.203) | data formatting | bytes 1048576
